TPU v7x, 32 devices: a whole 2x2x4 slice. The times are simulated.
32 devices in a mesh: dp: 8 (over y, x, core), ctx: 4 (over z).
Axes of the slice: x: 2, y: 2, z: 4, core: 2. Of those that a mesh axis runs over, the one named last changes fastest.
Arguments:
- tokens: bfloat16 [8, 32, 16, 3072], P('dp', 'ctx'), may hold values from -6 to 6
- modulation: float32 [8, 3, 3072], P('dp'), may hold values from -3 to 3
- query_key_value_weight: bfloat16 [3072, 1536], P('dp'), may hold values from -0.109375 to 0.109375
- output_projection_weight: bfloat16 [512, 3072], P(None, 'dp'), may hold values from -0.25 to 0.25
- adapter_down_maps: bfloat16 [3072, 64], P('dp'), may hold values from -0.109375 to 0.109375
- adapter_up_maps: bfloat16 [64, 512], P('dp'), may hold values from -1 to 1
- output_gradient: bfloat16 [8, 32, 16, 3072], P('dp', 'ctx'), may hold values from -6 to 6
Outputs:
- mixed_out: bfloat16 [8, 32, 16, 3072], P('dp', 'ctx')
- tokens_grad: bfloat16 [8, 32, 16, 3072], P('dp', 'ctx')
- modulation_grad: float32 [8, 3, 3072], P('dp')
- down_grad: float32 [3072, 64], P('dp')
- up_grad: float32 [64, 512], P('dp')
All inputs are finite; a program needn't handle non-finite values.
Results may differ from a plain program's by a relative error of at most 0.019.
Values may be sent and summed in bfloat16 or wider, within the bound.
A program may use at most 128 MiB of HBM per device.

v0:
```python
import functools

import jax
import jax.numpy as jnp
import numpy as np
from jax import lax
from jax.experimental import pallas as pl
from jax.experimental.pallas import tpu as pltpu
from jax.sharding import PartitionSpec as P

HEAD_SIZE = 128


EPSILON = 1e-06


def times_transposed(left, right):
    return lax.dot_general(
        left, right, (((1,), (1,)), ((), ())), preferred_element_type=jnp.float32
    )


def transposed_times(left, right):
    return lax.dot_general(
        left, right, (((0,), (0,)), ((), ())), preferred_element_type=jnp.float32
    )


def normalize_rows(flat_tokens, modulation_per_clip):
    values = flat_tokens.astype(jnp.float32)
    center = values - jnp.mean(values, -1, keepdims=True)
    inverse_value = lax.rsqrt(jnp.mean(center * center, -1, keepdims=True) + EPSILON)
    normalized_input = center * inverse_value
    hidden_state = (
        normalized_input * (1.0 + modulation_per_clip[1]) + modulation_per_clip[0]
    ).astype(jnp.bfloat16)
    return (normalized_input, inverse_value, hidden_state)


def projection_forward(hidden_state, qkv_full, down_full, up_full, adapter_inner_rank):
    head_size_value = up_full.shape[1]
    base_proj = jnp.dot(hidden_state, qkv_full, preferred_element_type=jnp.float32)
    low_rank_product = jnp.dot(hidden_state, down_full, preferred_element_type=jnp.float32).astype(
        jnp.bfloat16
    )
    delta_query = jnp.dot(
        low_rank_product[:, :adapter_inner_rank],
        up_full[:adapter_inner_rank],
        preferred_element_type=jnp.float32,
    )
    delta_value = jnp.dot(
        low_rank_product[:, adapter_inner_rank:],
        up_full[adapter_inner_rank:],
        preferred_element_type=jnp.float32,
    )
    query_unnormalized = base_proj[:, :head_size_value] + delta_query
    key_unnormalized = base_proj[:, head_size_value : 2 * head_size_value]
    value_row_matrix = (base_proj[:, 2 * head_size_value :] + delta_value).astype(jnp.bfloat16)
    return (low_rank_product, query_unnormalized, key_unnormalized, value_row_matrix)


def head_stats(raw_rows, head_dim):
    grouped = raw_rows.reshape(raw_rows.shape[0], -1, head_dim)
    inverse_value = lax.rsqrt(jnp.mean(grouped * grouped, -1, keepdims=True) + EPSILON)
    return (grouped, inverse_value)


def head_normed(raw_rows, head_dim):
    grouped, inverse_value = head_stats(raw_rows, head_dim)
    return (grouped * inverse_value).reshape(raw_rows.shape).astype(jnp.bfloat16)


def head_norm_back(raw_rows, incoming_grad, head_dim):
    grouped, inverse_value = head_stats(raw_rows, head_dim)
    incoming = incoming_grad.astype(jnp.float32).reshape(grouped.shape)
    inner_mean = jnp.mean(grouped * incoming, -1, keepdims=True)
    return (inverse_value * incoming - grouped * inverse_value**3 * inner_mean).reshape(
        raw_rows.shape
    )


def split_heads(rows_in, head_dim):
    frame_count, place_count, head_size_value = rows_in.shape
    return rows_in.reshape(frame_count, place_count, head_size_value // head_dim, head_dim)


def attend(query_rows, key_rows, value_row_matrix, head_dim):
    score_scale = head_dim ** (-0.5)
    query_heads = split_heads(query_rows, head_dim)
    key_heads = split_heads(key_rows, head_dim)
    value_heads = split_heads(value_row_matrix, head_dim)
    scores = (
        jnp.einsum("fphd,gphd->phfg", query_heads, key_heads, preferred_element_type=jnp.float32)
        * score_scale
    )
    expo = jnp.exp(scores)
    attention_weights = expo / jnp.sum(expo, -1, keepdims=True)
    weights_low = attention_weights.astype(jnp.bfloat16)
    attended = jnp.einsum(
        "phfg,gphd->fphd", weights_low, value_heads, preferred_element_type=jnp.float32
    ).astype(jnp.bfloat16)
    return (attended.reshape(query_rows.shape), attention_weights)


def attend_back(attended_grad, attention_weights, query_rows, key_rows, value_row_matrix, head_dim):
    score_scale = head_dim ** (-0.5)
    grad_heads = split_heads(attended_grad, head_dim)
    query_heads = split_heads(query_rows, head_dim)
    key_heads = split_heads(key_rows, head_dim)
    value_heads = split_heads(value_row_matrix, head_dim)
    weights_low = attention_weights.astype(jnp.bfloat16)
    prob_grad = jnp.einsum(
        "fphd,gphd->phfg", grad_heads, value_heads, preferred_element_type=jnp.float32
    )
    value_gradient = jnp.einsum(
        "phfg,fphd->gphd", weights_low, grad_heads, preferred_element_type=jnp.float32
    ).astype(jnp.bfloat16)
    score_grad = attention_weights * (
        prob_grad - jnp.sum(attention_weights * prob_grad, -1, keepdims=True)
    )
    score_low = (score_grad * score_scale).astype(jnp.bfloat16)
    query_grad = jnp.einsum(
        "phfg,gphd->fphd", score_low, key_heads, preferred_element_type=jnp.float32
    ).astype(jnp.bfloat16)
    key_grad = jnp.einsum(
        "phfg,fphd->gphd", score_low, query_heads, preferred_element_type=jnp.float32
    ).astype(jnp.bfloat16)
    shape_rows = query_rows.shape
    return (
        query_grad.reshape(shape_rows),
        key_grad.reshape(shape_rows),
        value_gradient.reshape(shape_rows),
    )


def projection_backward(
    query_normalized_gradient,
    key_normalized_gradient,
    value_gradient,
    query_unnormalized,
    key_unnormalized,
    hidden_state,
    low_rank_product,
    normalized_input,
    inverse_value,
    modulation_per_clip,
    qkv_full,
    down_full,
    up_full,
    adapter_inner_rank,
    head_dim,
):
    head_size_value = up_full.shape[1]
    query_back = head_norm_back(query_unnormalized, query_normalized_gradient, head_dim)
    key_back = head_norm_back(key_unnormalized, key_normalized_gradient, head_dim)
    joined_grad = jnp.concatenate(
        [query_back, key_back, value_gradient.astype(jnp.float32)], 1
    ).astype(jnp.bfloat16)
    query_block = joined_grad[:, :head_size_value]
    value_block = joined_grad[:, 2 * head_size_value :]
    up_grad = jnp.concatenate(
        [
            transposed_times(low_rank_product[:, :adapter_inner_rank], query_block),
            transposed_times(low_rank_product[:, adapter_inner_rank:], value_block),
        ],
        0,
    )
    low_grad = jnp.concatenate(
        [
            times_transposed(query_block, up_full[:adapter_inner_rank]),
            times_transposed(value_block, up_full[adapter_inner_rank:]),
        ],
        1,
    ).astype(jnp.bfloat16)
    hidden_grad = times_transposed(joined_grad, qkv_full) + times_transposed(low_grad, down_full)
    down_grad = transposed_times(hidden_state, low_grad)
    shift_gradient = jnp.sum(hidden_grad, 0)
    scale_gradient = jnp.sum(hidden_grad * normalized_input, 0)
    normed_grad = hidden_grad * (1.0 + modulation_per_clip[1])
    first_mean = jnp.mean(normed_grad, -1, keepdims=True)
    second_mean = jnp.mean(normed_grad * normalized_input, -1, keepdims=True)
    token_gradient_rows = inverse_value * (
        normed_grad - first_mean - normalized_input * second_mean
    )
    return (token_gradient_rows, shift_gradient, scale_gradient, down_grad, up_grad)


def per_device(
    tokens,
    modulation,
    query_key_value_weight,
    output_projection_weight,
    adapter_down_maps,
    adapter_up_maps,
    output_gradient,
):
    adapter_inner_rank = adapter_down_maps.shape[1] // 2
    head_dim = HEAD_SIZE
    qkv_full, out_full, down_full, up_full = (
        lax.all_gather(query_key_value_weight, "dp", axis=0, tiled=True),
        lax.all_gather(output_projection_weight, "dp", axis=1, tiled=True),
        lax.all_gather(adapter_down_maps, "dp", axis=0, tiled=True),
        lax.all_gather(adapter_up_maps, "dp", axis=0, tiled=True),
    )
    head_size_value = up_full.shape[1]
    local_shape = tokens.shape
    frame_shape = (1, local_shape[1], local_shape[2], head_size_value)
    modulation_per_clip = modulation[0]
    flat_tokens = tokens.reshape(-1, local_shape[3])
    normalized_input, inverse_value, hidden_state = normalize_rows(flat_tokens, modulation_per_clip)
    low_rank_product, query_unnormalized, key_unnormalized, value_row_matrix = projection_forward(
        hidden_state, qkv_full, down_full, up_full, adapter_inner_rank
    )
    query_rows = head_normed(query_unnormalized, head_dim)
    key_rows = head_normed(key_unnormalized, head_dim)
    upstream = output_gradient.reshape(-1, local_shape[3]).astype(jnp.float32)
    branch_grad = (upstream * modulation_per_clip[2]).astype(jnp.bfloat16)
    attended_grad = (
        times_transposed(branch_grad, out_full).astype(jnp.bfloat16).reshape(frame_shape)
    )
    query_place, key_place, value_place = (
        lax.all_to_all(
            query_rows.reshape(frame_shape), "ctx", split_axis=2, concat_axis=1, tiled=True
        ),
        lax.all_to_all(
            key_rows.reshape(frame_shape), "ctx", split_axis=2, concat_axis=1, tiled=True
        ),
        lax.all_to_all(
            value_row_matrix.reshape(frame_shape), "ctx", split_axis=2, concat_axis=1, tiled=True
        ),
    )
    attended, attention_weights = attend(query_place[0], key_place[0], value_place[0], head_dim)
    attended_frames = lax.all_to_all(attended[None], "ctx", split_axis=1, concat_axis=2, tiled=True)
    grad_place = lax.all_to_all(attended_grad, "ctx", split_axis=2, concat_axis=1, tiled=True)
    query_normalized_gradient, key_normalized_gradient, value_gradient = attend_back(
        grad_place[0], attention_weights, query_place[0], key_place[0], value_place[0], head_dim
    )
    query_back_frames, key_back_frames, value_back_frames = (
        lax.all_to_all(
            query_normalized_gradient[None], "ctx", split_axis=1, concat_axis=2, tiled=True
        ),
        lax.all_to_all(
            key_normalized_gradient[None], "ctx", split_axis=1, concat_axis=2, tiled=True
        ),
        lax.all_to_all(value_gradient[None], "ctx", split_axis=1, concat_axis=2, tiled=True),
    )
    branch_out = jnp.dot(
        attended_frames.reshape(-1, head_size_value), out_full, preferred_element_type=jnp.float32
    )
    mixed_out = (flat_tokens.astype(jnp.float32) + modulation_per_clip[2] * branch_out).astype(
        jnp.bfloat16
    )
    gate_grad = jnp.sum(upstream * branch_out, 0)
    token_gradient_rows, shift_gradient, scale_gradient, down_section, up_section = (
        projection_backward(
            query_back_frames.reshape(-1, head_size_value),
            key_back_frames.reshape(-1, head_size_value),
            value_back_frames.reshape(-1, head_size_value),
            query_unnormalized,
            key_unnormalized,
            hidden_state,
            low_rank_product,
            normalized_input,
            inverse_value,
            modulation_per_clip,
            qkv_full,
            down_full,
            up_full,
            adapter_inner_rank,
            head_dim,
        )
    )
    tokens_grad = (upstream + token_gradient_rows).astype(jnp.bfloat16)
    token_total = lax.axis_size("dp") * lax.axis_size("ctx") * flat_tokens.shape[0]
    grad_scale = token_total ** (-0.5)
    modulation_part = jnp.stack([shift_gradient, scale_gradient, gate_grad], 0)[None] * grad_scale
    down_section = down_section * grad_scale
    up_section = up_section * grad_scale
    down_total, up_total, modulation_grad = (
        lax.psum(down_section.astype(jnp.bfloat16), "ctx").astype(jnp.float32),
        lax.psum(up_section.astype(jnp.bfloat16), "ctx").astype(jnp.float32),
        lax.psum(modulation_part.astype(jnp.bfloat16), "ctx").astype(jnp.float32),
    )
    down_grad, up_grad = (
        lax.psum_scatter(
            down_total.astype(jnp.bfloat16), "dp", scatter_dimension=0, tiled=True
        ).astype(jnp.float32),
        lax.psum_scatter(
            up_total.astype(jnp.bfloat16), "dp", scatter_dimension=0, tiled=True
        ).astype(jnp.float32),
    )
    return (
        mixed_out.reshape(local_shape),
        tokens_grad.reshape(local_shape),
        modulation_grad,
        down_grad,
        up_grad,
    )


BF16 = jnp.bfloat16
F32 = jnp.float32


def dot_nn(a, b):
    return lax.dot_general(a, b, (((1,), (0,)), ((), ())), preferred_element_type=F32)


def place(y, x, c):
    return y * 4 + x * 2 + c


def layer_kernel(
    dims,
    tokens, modulation, outgrad, perm, perm_back, same_place, qkv_in, out_in, down_in, up_in,
    mixed_out, tokens_grad, mod_out, down_out, up_out,
    W, O, DT, U, H, N, BG, RAW, DS, DR, QS, QR, OS, OR, GS, GR,
    WT, LOW, JG, LG, HG, RS, RR, US, UR, ZD, ZU, ZM,
    local_sem, gs_sem, gr_sem, ds_sem, dr_sem, qs_sem, qr_sem, os_sem, or_sem,
    bs_sem, br_sem, rs_sem, rr_sem, us_sem, ur_sem, zs_sem, zr_sem,
):
    ndp, nctx, rows, width, block, heads_width, rank2, total_tokens = dims
    nh = heads_width // HEAD_SIZE
    part = rows // nctx
    qkv_width = 3 * heads_width
    me = lax.axis_index("dp")
    mz = lax.axis_index("ctx")
    y, x, c = me // 4, (me // 2) % 2, me % 2
    y1, x1, c1 = 1 - y, 1 - x, 1 - c
    xn, yn, pt = place(y, x1, c), place(y1, x, c), place(y, x, c1)
    rel_owner = place((y + c) % 2, (x + 1 - c) % 2, c)
    rel_target = place((y + 1 - c) % 2, (x + c) % 2, c)
    oth_owner = rel_target
    diag = place(y1, x1, c)
    rel_r = 2 + 2 * c
    oth_r = 4 - 2 * c

    barrier = pltpu.get_barrier_semaphore()
    for t in range(1, ndp):
        pl.semaphore_signal(barrier, inc=1, device_id={"dp": lax.rem(me + t, ndp)}, device_id_type=pl.DeviceIdType.MESH)
    for t in range(1, nctx):
        pl.semaphore_signal(barrier, inc=1, device_id={"ctx": lax.rem(mz + t, nctx)}, device_id_type=pl.DeviceIdType.MESH)
    pl.semaphore_wait(barrier, ndp - 1 + nctx - 1)

    parity = mz % 2
    pair_z = mz + 1 - 2 * parity
    big = (block // 16) * 5 // 24 * 16
    rest = block - 4 * big
    items, near = 8, 6

    def view(ref, own, k):
        if k == 2:
            return out_in if own else O.at[ref]
        if k == 3:
            return down_in if own else DT.at[ref]
        if k == 4:
            return up_in if own else U.at[ref]
        if k == 5:
            span = pl.ds(0, rest)
        elif k < 2:
            span = pl.ds(pl.multiple_of(rest + (2 * parity + k) * big, 16), big)
        else:
            span = pl.ds(pl.multiple_of(rest + (2 * (1 - parity) + k - near) * big, 16), big)
        return qkv_in.at[span, :] if own else W.at[ref, span, :]

    def piece(owner, k):
        return view(owner, False, k)

    def own_piece(k):
        return view(me, True, k)

    def push(src, owner, k, target, s, r):
        return pltpu.make_async_remote_copy(
            src_ref=src, dst_ref=piece(owner, k), send_sem=gs_sem.at[s, k], recv_sem=gr_sem.at[r, k],
            device_id={"dp": target}, device_id_type=pl.DeviceIdType.MESH)

    def across(owner, k, s, r):
        return pltpu.make_async_remote_copy(
            src_ref=piece(owner, k), dst_ref=piece(owner, k), send_sem=gs_sem.at[s, k],
            recv_sem=gr_sem.at[r, near + k],
            device_id={"ctx": pair_z}, device_id_type=pl.DeviceIdType.MESH)

    def arrived(owner, k, r):
        push(piece(owner, k), owner, k, pt, 0, r).wait_recv()

    def forward(owner, k, s, r):
        push(piece(owner, k), owner, k, pt, s, r).start()

    def own_out(k):
        push(own_piece(k), me, k, xn, 0, 2).start()
        push(own_piece(k), me, k, yn, 1, 4).start()

    locals_ = []
    for k in (0, 1, 2):
        own_out(k)
    for k in range(items):
        copy = pltpu.make_async_copy(own_piece(k), piece(me, k), local_sem.at[k])
        copy.start()
        locals_.append(copy)
        push(own_piece(k), me, k, pt, 2, 1).start()

    def cols(j):
        return pl.ds(pl.multiple_of(j * block, 128), block)

    def sum_body(j, s):
        return s + jnp.sum(tokens[:, cols(j)].astype(F32), -1, keepdims=True)

    mean = lax.fori_loop(0, ndp, sum_body, jnp.zeros((rows, 1), F32)) / width

    def var_body(j, s):
        d = tokens[:, cols(j)].astype(F32) - mean
        return s + jnp.sum(d * d, -1, keepdims=True)

    var = lax.fori_loop(0, ndp, var_body, jnp.zeros((rows, 1), F32)) / width
    rstd = lax.rsqrt(var + EPSILON)

    def norm_body(j, _):
        n = (tokens[:, cols(j)].astype(F32) - mean) * rstd
        N[j] = n
        H[j] = (n * (1.0 + modulation[1:2, cols(j)]) + modulation[0:1, cols(j)]).astype(BF16)
        BG[j] = (outgrad[:, cols(j)].astype(F32) * modulation[2:3, cols(j)]).astype(BF16)
        return 0

    lax.fori_loop(0, ndp, norm_body, 0)

    def from_sides(k):
        arrived(rel_owner, k, rel_r)
        push(piece(rel_owner, k), rel_owner, k, rel_target, 3, 6).start()
        if k < 2:
            across(rel_owner, k, 7, rel_r).start()
        forward(rel_owner, k, 4, 1 + rel_r)
        arrived(oth_owner, k, oth_r)
        if k < 2:
            across(oth_owner, k, 8, oth_r).start()
        forward(oth_owner, k, 5, 1 + oth_r)

    def from_diag(k):
        arrived(diag, k, 6)
        if k < 2:
            across(diag, k, 9, 6).start()
        forward(diag, k, 6, 7)

    pt_owners = ((pt, 1), (place(y, x1, c1), 3), (place(y1, x, c1), 5))
    last_owner = place(y1, x1, c1)

    def grad_part(owner):
        WT[...] += times_transposed(BG[owner], O[owner])

    def qkv_part(owner):
        RAW[...] += dot_nn(H[owner], W[owner])
        LOW[...] += dot_nn(H[owner], DT[owner])

    RAW[...] = jnp.zeros_like(RAW)
    LOW[...] = jnp.zeros_like(LOW)
    WT[...] = jnp.zeros_like(WT)
    for k in (0, 1):
        from_sides(k)
    for k in (3, 4, 5):
        own_out(k)
    for k in range(items):
        locals_[k].wait()
    grad_part(me)
    qkv_part(me)
    from_sides(2)
    for k in (0, 1):
        from_diag(k)
    for k in (3, 4, 5):
        from_sides(k)
    from_diag(2)
    for owner in (xn, yn):
        grad_part(owner)
    for owner, r in pt_owners:
        arrived(owner, 2, r)
        grad_part(owner)
    grad_part(diag)
    arrived(last_owner, 2, 7)
    grad_part(last_owner)

    def ctx_copy(src, dst, ssem, rsem, t):
        return pltpu.make_async_remote_copy(
            src_ref=src, dst_ref=dst, send_sem=ssem.at[t], recv_sem=rsem.at[t],
            device_id={"ctx": lax.rem(mz + t, nctx)}, device_id_type=pl.DeviceIdType.MESH)

    def exchange(sent, got, ssem, rsem):
        copies = []
        for t in range(1, nctx):
            copy = ctx_copy(sent.at[lax.rem(mz + t, nctx)], got.at[mz], ssem, rsem, t)
            copy.start()
            copies.append(copy)
        return copies

    def to_place(value):
        return dot_nn(perm[...], value).astype(BF16)

    def to_frame(value):
        return dot_nn(perm_back[...], value).astype(BF16)

    DS[...] = to_place(WT[...].astype(BF16)).reshape(nctx, part, heads_width)
    DR[mz] = DS[mz]
    grad_copies = exchange(DS, DR, ds_sem, dr_sem)

    for k in (near, near + 1):
        arrived(rel_owner, k, rel_r)
        forward(rel_owner, k, 4, 1 + rel_r)
        arrived(oth_owner, k, oth_r)
        forward(oth_owner, k, 5, 1 + oth_r)
    for owner in (xn, yn):
        qkv_part(owner)
    for owner, r in pt_owners:
        for k in range(items):
            if k != 2:
                arrived(owner, k, r)
        qkv_part(owner)
    for k in (3, 4, 5, near, near + 1):
        from_diag(k)
    qkv_part(diag)
    for k in range(items):
        if k != 2:
            arrived(last_owner, k, 7)
    qkv_part(last_owner)

    up_rows = U[...].astype(F32).reshape(rank2, heads_width)
    in_query = lax.broadcasted_iota(jnp.int32, (rank2, heads_width), 0) < rank2 // 2
    up_query = jnp.where(in_query, up_rows, 0.0).astype(BF16)
    up_value = jnp.where(in_query, 0.0, up_rows).astype(BF16)
    low = LOW[...].astype(BF16)
    RAW[:, :heads_width] += dot_nn(low, up_query)
    RAW[:, 2 * heads_width :] += dot_nn(low, up_value)

    def head(h, section=0):
        lo = section * heads_width + h * HEAD_SIZE
        return slice(lo, lo + HEAD_SIZE)

    def inverse_of(raw):
        return lax.rsqrt(jnp.mean(raw * raw, -1, keepdims=True) + EPSILON)

    for section in range(3):
        for h in range(nh):
            raw = RAW[:, head(h, section)]
            if section < 2:
                raw = raw * inverse_of(raw)
            QS[:, :, head(h, section)] = to_place(raw.astype(BF16)).reshape(nctx, part, HEAD_SIZE)
    QR[mz] = QS[mz]
    qkv_copies = exchange(QS, QR, qs_sem, qr_sem)
    for copy in grad_copies:
        copy.wait()
    for copy in qkv_copies:
        copy.wait()

    scale = HEAD_SIZE ** (-0.5)
    same = same_place[...]

    def whole(ref, where):
        return ref[:, :, where].reshape(rows, HEAD_SIZE)

    weights = []
    for h in range(nh):
        q, k = whole(QR, head(h)), whole(QR, head(h, 1))
        v = whole(QR, head(h, 2))
        expo = jnp.exp(times_transposed(q, k) * scale) * same
        a = expo / jnp.sum(expo, -1, keepdims=True)
        OS[:, :, head(h)] = dot_nn(a.astype(BF16), v).astype(BF16).reshape(nctx, part, HEAD_SIZE)
        weights.append(a)
    OR[mz] = OS[mz]
    out_copies = exchange(OS, OR, os_sem, or_sem)
    for h in range(nh):
        q, k = whole(QR, head(h)), whole(QR, head(h, 1))
        v, g = whole(QR, head(h, 2)), whole(DR, head(h))
        a = weights[h]
        dv = transposed_times(a.astype(BF16), g)
        dp = times_transposed(g, v)
        ds = (a * (dp - jnp.sum(a * dp, -1, keepdims=True)) * scale).astype(BF16)
        dq = dot_nn(ds, k)
        dk = transposed_times(ds, q)
        for section, value in enumerate((dq, dk, dv)):
            GS[:, :, head(h, section)] = value.astype(BF16).reshape(nctx, part, HEAD_SIZE)
    GR[mz] = GS[mz]
    back_copies = exchange(GS, GR, bs_sem, br_sem)

    grad_scale = total_tokens ** (-0.5)
    for copy in out_copies:
        copy.wait()
    OS[...] = to_frame(OR[...].reshape(rows, heads_width)).reshape(nctx, part, heads_width)

    def out_body(j, _):
        branch = dot_nn(OS[...].reshape(rows, heads_width), O[j])
        up = outgrad[:, cols(j)].astype(F32)
        mixed_out[:, cols(j)] = (
            tokens[:, cols(j)].astype(F32) + modulation[2:3, cols(j)] * branch
        ).astype(BF16)
        ZM[mz, 2, pl.ds(j, 1), :] = jnp.sum(up * branch, 0, keepdims=True) * grad_scale
        return 0

    lax.fori_loop(0, ndp, out_body, 0)

    for copy in back_copies:
        copy.wait()
    for section in range(3):
        for h in range(nh):
            where = head(h, section)
            u = to_frame(whole(GR, where))
            if section < 2:
                raw = RAW[:, where]
                inv = inverse_of(raw)
                uf = u.astype(F32)
                inner = jnp.mean(raw * uf, -1, keepdims=True)
                u = (inv * uf - raw * (inv * inv * inv) * inner).astype(BF16)
            JG[:, where] = u
    jq, jv = JG[:, :heads_width], JG[:, 2 * heads_width :]
    LG[...] = (times_transposed(jq, up_query) + times_transposed(jv, up_value)).astype(BF16)
    up_part = jnp.where(in_query, transposed_times(low, jq), transposed_times(low, jv)) * grad_scale
    US[...] = up_part.reshape(ndp, rank2 // ndp, heads_width)

    def down_body(j, _):
        RS[j] = (transposed_times(LG[...], H[j]) * grad_scale).astype(BF16)
        return 0

    lax.fori_loop(0, ndp, down_body, 0)
    reduce_copies = []
    for t in range(1, ndp):
        to = lax.rem(me + t, ndp)
        for src, dst, ss, rs in ((RS, RR, rs_sem, rr_sem), (US, UR, us_sem, ur_sem)):
            copy = pltpu.make_async_remote_copy(
                src_ref=src.at[to], dst_ref=dst.at[t], send_sem=ss.at[t], recv_sem=rs.at[t],
                device_id={"dp": to}, device_id_type=pl.DeviceIdType.MESH)
            copy.start()
            reduce_copies.append(copy)

    def hidden_body(j, sums):
        first, second = sums
        hg = times_transposed(JG[...], W[j]) + times_transposed(LG[...], DT[j])
        n = N[j]
        ZM[mz, 0, pl.ds(j, 1), :] = jnp.sum(hg, 0, keepdims=True) * grad_scale
        ZM[mz, 1, pl.ds(j, 1), :] = jnp.sum(hg * n, 0, keepdims=True) * grad_scale
        ng = hg * (1.0 + modulation[1:2, cols(j)])
        HG[j] = ng
        return (
            first + jnp.sum(ng, -1, keepdims=True),
            second + jnp.sum(ng * n, -1, keepdims=True),
        )

    zero = jnp.zeros((rows, 1), F32)
    first, second = lax.fori_loop(0, ndp, hidden_body, (zero, zero))
    z_copies = []

    def share(ref, row):
        for t in range(1, nctx):
            copy = ctx_copy(ref.at[mz], ref.at[mz], zs_sem.at[row], zr_sem.at[row], t)
            copy.start()
            z_copies.append(copy)

    share(ZM, 0)
    for copy in reduce_copies:
        copy.wait()
    down_sum = RS[me].astype(F32)
    up_sum = US[me]
    for t in range(1, ndp):
        down_sum = down_sum + RR[t].astype(F32)
        up_sum = up_sum + UR[t]
    ZD[mz] = down_sum.astype(BF16)
    ZU[mz] = up_sum
    share(ZD, 1)
    share(ZU, 2)

    first, second = first / width, second / width

    def last_body(j, _):
        grad = outgrad[:, cols(j)].astype(F32) + rstd * (HG[j] - first - N[j] * second)
        tokens_grad[:, cols(j)] = grad.astype(BF16)
        return 0

    lax.fori_loop(0, ndp, last_body, 0)
    for copy in z_copies:
        copy.wait()
    down_all, up_all, mod_all = ZD[0].astype(F32), ZU[0], ZM[0]
    for z in range(1, nctx):
        down_all = down_all + ZD[z].astype(F32)
        up_all = up_all + ZU[z]
        mod_all = mod_all + ZM[z]
    down_out[...] = down_all.T
    up_out[...] = up_all
    for j in range(ndp):
        mod_out[:, j * block : (j + 1) * block] = mod_all[:, j, :]

    for k in range(items):
        used = range(10) if k < 2 else range(7) if k < near else (2, 4, 5, 6)
        for s in used:
            push(piece(me, k), me, k, pt, s, 1).wait_send()


def per_device_kernel(mesh_shape, *args):
    ndp, nctx = mesh_shape
    tokens, modulation, qkv, out, down, up, outgrad = args
    _, frames, places, width = tokens.shape
    rows = frames * places
    block = width // ndp
    rank2 = down.shape[1]
    hw = up.shape[1]
    part = rows // nctx
    order = np.arange(rows).reshape(frames, places).T.reshape(-1)
    perm = np.zeros((rows, rows), np.float32)
    perm[np.arange(rows), order] = 1.0
    which = (np.arange(rows) // frames) % (places // nctx)
    same = (which[:, None] == which[None, :]).astype(np.float32)
    dims = (ndp, nctx, rows, width, block, hw, rank2, ndp * nctx * rows)
    vm = pl.BlockSpec(memory_space=pltpu.VMEM)
    hbm = pl.BlockSpec(memory_space=pltpu.HBM)
    sem = pltpu.SemaphoreType.DMA
    ur = rank2 // ndp
    scratch = [
        pltpu.VMEM((ndp, block, 3 * hw), BF16),
        pltpu.VMEM((ndp, hw, block), BF16),
        pltpu.VMEM((ndp, block, rank2), BF16),
        pltpu.VMEM((ndp, ur, hw), BF16),
        pltpu.VMEM((ndp, rows, block), BF16),
        pltpu.VMEM((ndp, rows, block), F32),
        pltpu.VMEM((ndp, rows, block), BF16),
        pltpu.VMEM((rows, 3 * hw), F32),
    ]
    for w in (hw, 3 * hw, hw, 3 * hw):
        scratch += [pltpu.VMEM((nctx, part, w), BF16)] * 2
    scratch += [
        pltpu.VMEM((rows, hw), F32),
        pltpu.VMEM((rows, rank2), F32),
        pltpu.VMEM((rows, 3 * hw), BF16),
        pltpu.VMEM((rows, rank2), BF16),
        pltpu.VMEM((ndp, rows, block), F32),
        pltpu.VMEM((ndp, rank2, block), BF16),
        pltpu.VMEM((ndp, rank2, block), BF16),
        pltpu.VMEM((ndp, ur, hw), F32),
        pltpu.VMEM((ndp, ur, hw), F32),
        pltpu.VMEM((nctx, rank2, block), BF16),
        pltpu.VMEM((nctx, ur, hw), F32),
        pltpu.VMEM((nctx, 3, ndp, block), F32),
        sem((8,)),
        sem((10, 8)),
        sem((8, 8)),
    ]
    scratch += [sem((nctx,))] * 8 + [sem((ndp,))] * 4 + [sem((3, nctx))] * 2
    results = pl.pallas_call(
        functools.partial(layer_kernel, dims),
        out_shape=(
            jax.ShapeDtypeStruct((rows, width), BF16),
            jax.ShapeDtypeStruct((rows, width), BF16),
            jax.ShapeDtypeStruct((3, width), F32),
            jax.ShapeDtypeStruct((block, rank2), F32),
            jax.ShapeDtypeStruct((ur, hw), F32),
        ),
        in_specs=[vm] * 6 + [hbm] * 4,
        out_specs=[vm] * 5,
        scratch_shapes=scratch,
        compiler_params=pltpu.CompilerParams(
            collective_id=0, has_side_effects=True, vmem_limit_bytes=60 * 1024 * 1024
        ),
    )(
        tokens.reshape(rows, width),
        modulation[0],
        outgrad.reshape(rows, width),
        jnp.asarray(perm, BF16),
        jnp.asarray(perm.T, BF16),
        jnp.asarray(same, F32),
        qkv,
        out,
        down,
        up,
    )
    mixed, tgrad, mod, dgrad, ugrad = results
    return mixed.reshape(tokens.shape), tgrad.reshape(tokens.shape), mod[None], dgrad, ugrad


def solution(mesh):
    ndp, nctx = mesh.shape["dp"], mesh.shape["ctx"]
    body = functools.partial(per_device_kernel, (ndp, nctx)) if ndp == 8 and nctx % 2 == 0 else per_device
    return jax.shard_map(
        body,
        mesh=mesh,
        in_specs=(
            P("dp", "ctx", None, None),
            P("dp", None, None),
            P("dp", None),
            P(None, "dp"),
            P("dp", None),
            P("dp", None),
            P("dp", "ctx", None, None),
        ),
        out_specs=(
            P("dp", "ctx", None, None),
            P("dp", "ctx", None, None),
            P("dp", None, None),
            P("dp", None),
            P("dp", None),
        ),
        check_vma=False,
    )
```

profile of v0, /device:TPU:0, one launch (start us, length us, event | category | flops | bytes accessed | tf_op | source)
XLA Modules:
  0.0 105.5 jit_solution(12432319891360784514)
XLA Ops:
  0.6 1.4 %copy.20 = f32[1,3,3072]{2,1,0:T(4,128)} copy(f32[1,3,3072]{2,0,1:T(1,128)} %param.11) | data formatting | bytes 73728
  2.0 1.5 %copy.15.down_in = bf16[384,64]{1,0:T(8,128)(2,1)} copy(bf16[384,64]{0,1:T(8,128)(2,1)} %param.14) | data formatting | bytes 98304 | tf_op args[4]
  3.6 95.1 %shard_map.137 = (bf16[128,3072]{1,0:T(8,128)(2,1)}, bf16[128,3072]{1,0:T(8,128)(2,1)}, f32[3,3072]{1,0:T(4,128)}, f32[384,64]{1,0:T(8,128)}, f32[8,512]{1,0:T(8,128)}) custom-call(bf16[128,3072]{1,0:T(8,128)(2,1)} %bitcast.10, f32[3,3072]{1,0:T(4,128)} %bitcast.12, bf16[128,3072]{1,0:T(8,128)(2,1)} %bitcast.11, bf16[128,128]{1,0:T(8,128)(2,1)} %constant.6.clone.perm, ...), custom_call_target="tpu_custom_call" | custom-call | tf_op jit(solution)/shard_map/pallas_call | solution.py:740
  98.7 0.0 copy-start
  98.7 1.5 %copy.16 = f32[1,3,3072]{2,0,1:T(1,128)} copy(f32[1,3,3072]{2,1,0:T(4,128)} %bitcast.13) | data formatting | bytes 73728
  100.2 1.7 %copy.17 = f32[384,64]{0,1:T(8,128)} copy(f32[384,64]{1,0:T(8,128)} %get-tuple-element.18) | data formatting | bytes 196608
  101.9 0.0 copy-start.1
  101.9 2.1 %copy.24 = bf16[1,8,16,3072]{3,2,1,0:T(8,128)(2,1)} copy(bf16[1,8,16,3072]{3,2,1,0:T(8,128)(2,1)} %bitcast.9) | data formatting | bytes 1572864
  104.0 0.0 copy-done
  104.0 0.9 copy.25
  104.8 0.0 copy-done.1
  104.9 0.6 copy.26
Async XLA Ops:
  98.7 5.3 %copy-start = (bf16[128,3072]{1,0:T(8,128)(2,1)S(1)}, bf16[128,3072]{1,0:T(8,128)(2,1)}, u32[]{:S(2)}) copy-start(bf16[128,3072]{1,0:T(8,128)(2,1)} %get-tuple-element.11) | copy-start | bytes 2359300
  101.9 3.0 %copy-start.1 = (f32[8,512]{1,0:T(8,128)S(1)}, f32[8,512]{1,0:T(8,128)}, u32[]{:S(2)}) copy-start(f32[8,512]{1,0:T(8,128)} %get-tuple-element.29) | copy-start | bytes 49156
where the time goes:
time: 106 us; the launch traced here: 105 us
  Pallas kernels  95.1 us (90%)
  local copies, waits for them, and re-layouts  9.72 us (9%)
    pallas_call x1, Pallas kernels, per_device_kernel(): pl.pallas_call(functools.partial(layer_kernel, dims), out_shape=(jax.Shap...  95.1 us
    unnamed x11, local copies, waits for them, and re-layouts  9.72 us

commit v1 on v0

--- a/solution.py
+++ b/solution.py
@@ -2,7 +2,6 @@
 
 import jax
 import jax.numpy as jnp
-import numpy as np
 from jax import lax
 from jax.experimental import pallas as pl
 from jax.experimental.pallas import tpu as pltpu
@@ -312,14 +311,14 @@
 
 def layer_kernel(
     dims,
-    tokens, modulation, outgrad, perm, perm_back, same_place, qkv_in, out_in, down_in, up_in,
+    tokens_in, modulation_in, outgrad_in, qkv_in, out_in, down_in, up_in,
     mixed_out, tokens_grad, mod_out, down_out, up_out,
-    W, O, DT, U, H, N, BG, RAW, DS, DR, QS, QR, OS, OR, GS, GR,
+    tokens, modulation, outgrad, W, O, DT, U, H, N, BG, RAW, DS, DR, QS, QR, OS, OR, GS, GR,
     WT, LOW, JG, LG, HG, RS, RR, US, UR, ZD, ZU, ZM,
-    local_sem, gs_sem, gr_sem, ds_sem, dr_sem, qs_sem, qr_sem, os_sem, or_sem,
+    load_sem, local_sem, gs_sem, gr_sem, ds_sem, dr_sem, qs_sem, qr_sem, os_sem, or_sem,
     bs_sem, br_sem, rs_sem, rr_sem, us_sem, ur_sem, zs_sem, zr_sem,
 ):
-    ndp, nctx, rows, width, block, heads_width, rank2, total_tokens = dims
+    ndp, nctx, rows, places, width, block, heads_width, rank2, total_tokens = dims
     nh = heads_width // HEAD_SIZE
     part = rows // nctx
     qkv_width = 3 * heads_width
@@ -340,6 +339,11 @@
         pl.semaphore_signal(barrier, inc=1, device_id={"dp": lax.rem(me + t, ndp)}, device_id_type=pl.DeviceIdType.MESH)
     for t in range(1, nctx):
         pl.semaphore_signal(barrier, inc=1, device_id={"ctx": lax.rem(mz + t, nctx)}, device_id_type=pl.DeviceIdType.MESH)
+    loads = []
+    for t, (src, dst) in enumerate(((tokens_in, tokens), (outgrad_in, outgrad), (modulation_in, modulation))):
+        load = pltpu.make_async_copy(src, dst, load_sem.at[t])
+        load.start()
+        loads.append(load)
     pl.semaphore_wait(barrier, ndp - 1 + nctx - 1)
 
     parity = mz % 2
@@ -402,6 +406,9 @@
     def cols(j):
         return pl.ds(pl.multiple_of(j * block, 128), block)
 
+    for load in loads:
+        load.wait()
+
     def sum_body(j, s):
         return s + jnp.sum(tokens[:, cols(j)].astype(F32), -1, keepdims=True)
 
@@ -417,8 +424,8 @@
     def norm_body(j, _):
         n = (tokens[:, cols(j)].astype(F32) - mean) * rstd
         N[j] = n
-        H[j] = (n * (1.0 + modulation[1:2, cols(j)]) + modulation[0:1, cols(j)]).astype(BF16)
-        BG[j] = (outgrad[:, cols(j)].astype(F32) * modulation[2:3, cols(j)]).astype(BF16)
+        H[j] = (n * (1.0 + modulation[1, :, cols(j)]) + modulation[0, :, cols(j)]).astype(BF16)
+        BG[j] = (outgrad[:, cols(j)].astype(F32) * modulation[2, :, cols(j)]).astype(BF16)
         return 0
 
     lax.fori_loop(0, ndp, norm_body, 0)
@@ -448,7 +455,7 @@
 
     def qkv_part(owner):
         RAW[...] += dot_nn(H[owner], W[owner])
-        LOW[...] += dot_nn(H[owner], DT[owner])
+        LOW[...] += times_transposed(H[owner], DT[owner])
 
     RAW[...] = jnp.zeros_like(RAW)
     LOW[...] = jnp.zeros_like(LOW)
@@ -489,11 +496,25 @@
             copies.append(copy)
         return copies
 
+    frames = rows // places
+    across_rows = lax.broadcasted_iota(jnp.int32, (rows, rows), 0)
+    along_rows = lax.broadcasted_iota(jnp.int32, (rows, rows), 1)
+    perm = jnp.where(
+        along_rows == (across_rows % frames) * places + across_rows // frames, 1.0, 0.0
+    ).astype(BF16)
+    perm_back = jnp.where(
+        across_rows == (along_rows % frames) * places + along_rows // frames, 1.0, 0.0
+    ).astype(BF16)
+    local_places = places // nctx
+    same = jnp.where(
+        (across_rows // frames) % local_places == (along_rows // frames) % local_places, 1.0, 0.0
+    )
+
     def to_place(value):
-        return dot_nn(perm[...], value).astype(BF16)
+        return dot_nn(perm, value).astype(BF16)
 
     def to_frame(value):
-        return dot_nn(perm_back[...], value).astype(BF16)
+        return dot_nn(perm_back, value).astype(BF16)
 
     DS[...] = to_place(WT[...].astype(BF16)).reshape(nctx, part, heads_width)
     DR[mz] = DS[mz]
@@ -548,7 +569,6 @@
         copy.wait()
 
     scale = HEAD_SIZE ** (-0.5)
-    same = same_place[...]
 
     def whole(ref, where):
         return ref[:, :, where].reshape(rows, HEAD_SIZE)
@@ -586,7 +606,7 @@
         branch = dot_nn(OS[...].reshape(rows, heads_width), O[j])
         up = outgrad[:, cols(j)].astype(F32)
         mixed_out[:, cols(j)] = (
-            tokens[:, cols(j)].astype(F32) + modulation[2:3, cols(j)] * branch
+            tokens[:, cols(j)].astype(F32) + modulation[2, :, cols(j)] * branch
         ).astype(BF16)
         ZM[mz, 2, pl.ds(j, 1), :] = jnp.sum(up * branch, 0, keepdims=True) * grad_scale
         return 0
@@ -628,11 +648,11 @@
 
     def hidden_body(j, sums):
         first, second = sums
-        hg = times_transposed(JG[...], W[j]) + times_transposed(LG[...], DT[j])
+        hg = times_transposed(JG[...], W[j]) + dot_nn(LG[...], DT[j])
         n = N[j]
         ZM[mz, 0, pl.ds(j, 1), :] = jnp.sum(hg, 0, keepdims=True) * grad_scale
         ZM[mz, 1, pl.ds(j, 1), :] = jnp.sum(hg * n, 0, keepdims=True) * grad_scale
-        ng = hg * (1.0 + modulation[1:2, cols(j)])
+        ng = hg * (1.0 + modulation[1, :, cols(j)])
         HG[j] = ng
         return (
             first + jnp.sum(ng, -1, keepdims=True),
@@ -677,15 +697,25 @@
         down_all = down_all + ZD[z].astype(F32)
         up_all = up_all + ZU[z]
         mod_all = mod_all + ZM[z]
-    down_out[...] = down_all.T
+    down_out[...] = down_all
     up_out[...] = up_all
     for j in range(ndp):
-        mod_out[:, j * block : (j + 1) * block] = mod_all[:, j, :]
+        for i in range(3):
+            mod_out[i, :, j * block : (j + 1) * block] = mod_all[i, j : j + 1, :]
 
     for k in range(items):
         used = range(10) if k < 2 else range(7) if k < near else (2, 4, 5, 6)
         for s in used:
             push(piece(me, k), me, k, pt, s, 1).wait_send()
+
+
+def finish_kernel(*refs):
+    sem = refs[10]
+    copies = [pltpu.make_async_copy(refs[i], refs[5 + i], sem.at[i]) for i in range(5)]
+    for copy in copies:
+        copy.start()
+    for copy in copies:
+        copy.wait()
 
 
 def per_device_kernel(mesh_shape, *args):
@@ -697,20 +727,18 @@
     rank2 = down.shape[1]
     hw = up.shape[1]
     part = rows // nctx
-    order = np.arange(rows).reshape(frames, places).T.reshape(-1)
-    perm = np.zeros((rows, rows), np.float32)
-    perm[np.arange(rows), order] = 1.0
-    which = (np.arange(rows) // frames) % (places // nctx)
-    same = (which[:, None] == which[None, :]).astype(np.float32)
-    dims = (ndp, nctx, rows, width, block, hw, rank2, ndp * nctx * rows)
+    dims = (ndp, nctx, rows, places, width, block, hw, rank2, ndp * nctx * rows)
     vm = pl.BlockSpec(memory_space=pltpu.VMEM)
     hbm = pl.BlockSpec(memory_space=pltpu.HBM)
     sem = pltpu.SemaphoreType.DMA
     ur = rank2 // ndp
     scratch = [
+        pltpu.VMEM((rows, width), BF16),
+        pltpu.VMEM((3, 1, width), F32),
+        pltpu.VMEM((rows, width), BF16),
         pltpu.VMEM((ndp, block, 3 * hw), BF16),
         pltpu.VMEM((ndp, hw, block), BF16),
-        pltpu.VMEM((ndp, block, rank2), BF16),
+        pltpu.VMEM((ndp, rank2, block), BF16),
         pltpu.VMEM((ndp, ur, hw), BF16),
         pltpu.VMEM((ndp, rows, block), BF16),
         pltpu.VMEM((ndp, rows, block), F32),
@@ -732,6 +760,7 @@
         pltpu.VMEM((nctx, rank2, block), BF16),
         pltpu.VMEM((nctx, ur, hw), F32),
         pltpu.VMEM((nctx, 3, ndp, block), F32),
+        sem((3,)),
         sem((8,)),
         sem((10, 8)),
         sem((8, 8)),
@@ -740,32 +769,48 @@
     results = pl.pallas_call(
         functools.partial(layer_kernel, dims),
         out_shape=(
-            jax.ShapeDtypeStruct((rows, width), BF16),
-            jax.ShapeDtypeStruct((rows, width), BF16),
-            jax.ShapeDtypeStruct((3, width), F32),
-            jax.ShapeDtypeStruct((block, rank2), F32),
-            jax.ShapeDtypeStruct((ur, hw), F32),
-        ),
-        in_specs=[vm] * 6 + [hbm] * 4,
+            pltpu.VMEM((rows, width), BF16),
+            pltpu.VMEM((rows, width), BF16),
+            pltpu.VMEM((3, 1, width), F32),
+            pltpu.VMEM((rank2, block), F32),
+            pltpu.VMEM((ur, hw), F32),
+        ),
+        in_specs=[hbm] * 7,
         out_specs=[vm] * 5,
         scratch_shapes=scratch,
         compiler_params=pltpu.CompilerParams(
-            collective_id=0, has_side_effects=True, vmem_limit_bytes=60 * 1024 * 1024
+            collective_id=0, has_side_effects=True, vmem_limit_bytes=52 * 1024 * 1024
         ),
     )(
         tokens.reshape(rows, width),
-        modulation[0],
+        pltpu.with_memory_space_constraint(modulation.reshape(3, 1, width), pltpu.HBM),
         outgrad.reshape(rows, width),
-        jnp.asarray(perm, BF16),
-        jnp.asarray(perm.T, BF16),
-        jnp.asarray(same, F32),
         qkv,
         out,
-        down,
-        up,
-    )
-    mixed, tgrad, mod, dgrad, ugrad = results
-    return mixed.reshape(tokens.shape), tgrad.reshape(tokens.shape), mod[None], dgrad, ugrad
+        pltpu.with_memory_space_constraint(down.T, pltpu.HBM),
+        pltpu.with_memory_space_constraint(up, pltpu.HBM),
+    )
+    mixed, tgrad, mod, dgrad, ugrad = pl.pallas_call(
+        finish_kernel,
+        out_shape=(
+            jax.ShapeDtypeStruct((rows, width), BF16),
+            jax.ShapeDtypeStruct((rows, width), BF16),
+            jax.ShapeDtypeStruct((3, 1, width), F32),
+            jax.ShapeDtypeStruct((rank2, block), F32),
+            jax.ShapeDtypeStruct((ur, hw), F32),
+        ),
+        in_specs=[vm] * 5,
+        out_specs=[hbm] * 5,
+        scratch_shapes=[sem((5,))],
+        compiler_params=pltpu.CompilerParams(vmem_limit_bytes=4 * 1024 * 1024),
+    )(*results)
+    return (
+        mixed.reshape(tokens.shape),
+        tgrad.reshape(tokens.shape),
+        mod.reshape(1, 3, width),
+        dgrad.T,
+        ugrad,
+    )
 
 
 def solution(mesh):

time: 106 us -> 93.2 us (0.88)
  local copies, waits for them, and re-layouts: 9.72 us -> 0 us
  Pallas kernels: 95.1 us -> 92.4 us
    unnamed x11 -> x0, local copies, waits for them, and re-layouts: 9.72 us -> none
    pallas_call x1 -> x2, Pallas kernels: 95.1 us -> 92.4 us  [the longest x1 91.2 us: per_device_kernel(): pl.pallas_call(functools.partial(layer_kernel, dims), out_shape=(pltpu.VM...]
where the time goes in v1:
time: 93.2 us; the launch traced here: 93 us
  Pallas kernels  92.4 us (99%)
    pallas_call x1, Pallas kernels, per_device_kernel(): pl.pallas_call(functools.partial(layer_kernel, dims), out_shape=(pltpu.VM...  91.2 us

profile of v1, /device:TPU:0, one launch (start us, length us, event | category | flops | bytes accessed | tf_op | source)
XLA Modules:
  0.0 93.0 jit_solution(873709807109090762)
XLA Ops:
  0.6 91.2 %shard_map.110 = (bf16[128,3072]{1,0:T(8,128)(2,1)S(1)}, bf16[128,3072]{1,0:T(8,128)(2,1)S(1)}, f32[3,1,3072]{2,1,0:T(1,128)S(1)}, f32[64,384]{1,0:T(8,128)S(1)}, f32[8,512]{1,0:T(8,128)S(1)}) custom-call(bf16[128,3072]{1,0:T(8,128)(2,1)} %bitcast.8, f32[3,1,3072]{2,1,0:T(1,128)} %bitcast.11, bf16[128,3072]{1,0:T(8,128)(2,1)} %bitcast.9, ...), custom_call_target="tpu_custom_call" | custom-call | tf_op jit(solution)/shard_map/pallas_call | solution.py:769
  91.8 1.2 %shard_map.111 = (bf16[128,3072]{1,0:T(8,128)(2,1)}, bf16[128,3072]{1,0:T(8,128)(2,1)}, f32[3,1,3072]{2,1,0:T(1,128)}, f32[64,384]{1,0:T(8,128)}, f32[8,512]{1,0:T(8,128)}) custom-call(bf16[128,3072]{1,0:T(8,128)(2,1)S(1)} %get-tuple-element.15.refs_0_, bf16[128,3072]{1,0:T(8,128)(2,1)S(1)} %get-tuple-element.16.refs_1_, ...), custom_call_target="tpu_custom_call" | custom-call | tf_op jit(solution)/shard_map/pallas_call | solution.py:793

commit v2 on v1

--- a/solution.py
+++ b/solution.py
@@ -305,6 +305,10 @@
     return lax.dot_general(a, b, (((1,), (0,)), ((), ())), preferred_element_type=F32)
 
 
+GROUPS = 2
+SHARED_ROWS = 16
+
+
 def place(y, x, c):
     return y * 4 + x * 2 + c
 
@@ -314,14 +318,15 @@
     tokens_in, modulation_in, outgrad_in, qkv_in, out_in, down_in, up_in,
     mixed_out, tokens_grad, mod_out, down_out, up_out,
     tokens, modulation, outgrad, W, O, DT, U, H, N, BG, RAW, DS, DR, QS, QR, OS, OR, GS, GR,
-    WT, LOW, JG, LG, HG, RS, RR, US, UR, ZD, ZU, ZM,
+    WT, LOW, LT, JG, LG, LGT, HG, AW, OF, RS, RR, US, UR, ZD, ZU, ZM, ZL,
     load_sem, local_sem, gs_sem, gr_sem, ds_sem, dr_sem, qs_sem, qr_sem, os_sem, or_sem,
     bs_sem, br_sem, rs_sem, rr_sem, us_sem, ur_sem, zs_sem, zr_sem,
 ):
     ndp, nctx, rows, places, width, block, heads_width, rank2, total_tokens = dims
     nh = heads_width // HEAD_SIZE
     part = rows // nctx
-    qkv_width = 3 * heads_width
+    gw = heads_width // GROUPS
+    per_group = nh // GROUPS
     me = lax.axis_index("dp")
     mz = lax.axis_index("ctx")
     y, x, c = me // 4, (me // 2) % 2, me % 2
@@ -339,75 +344,108 @@
         pl.semaphore_signal(barrier, inc=1, device_id={"dp": lax.rem(me + t, ndp)}, device_id_type=pl.DeviceIdType.MESH)
     for t in range(1, nctx):
         pl.semaphore_signal(barrier, inc=1, device_id={"ctx": lax.rem(mz + t, nctx)}, device_id_type=pl.DeviceIdType.MESH)
+
+    parity = mz % 2
+    pair_z = mz + 1 - 2 * parity
+    big = block // 48 * SHARED_ROWS
+    rest = block - 2 * big
+    NEAR, REST, FAR = (0, 3), (1, 4), (2, 5)
+    DOWN, UP = 6, 7
+    OUT = tuple(range(8, 8 + nh))
+    items = 8 + nh
+
+    def piece(owner, k):
+        if k in OUT:
+            return O.at[owner, pl.ds((k - OUT[0]) * HEAD_SIZE, HEAD_SIZE), :]
+        if k == DOWN:
+            return DT.at[owner]
+        if k == UP:
+            return U.at[owner]
+        if k in REST:
+            span = pl.ds(0, rest)
+        else:
+            side = parity if k in NEAR else 1 - parity
+            span = pl.ds(pl.multiple_of(rest + side * big, 16), big)
+        return W.at[owner, k // 3, span, :]
+
+    def push(owner, k, target, s, r):
+        return pltpu.make_async_remote_copy(
+            src_ref=piece(owner, k), dst_ref=piece(owner, k), send_sem=gs_sem.at[s, k],
+            recv_sem=gr_sem.at[r, k],
+            device_id={"dp": target}, device_id_type=pl.DeviceIdType.MESH)
+
+    def across(owner, k, s, r):
+        pltpu.make_async_remote_copy(
+            src_ref=piece(owner, k), dst_ref=piece(owner, k), send_sem=gs_sem.at[s, k],
+            recv_sem=gr_sem.at[r, k + 2],
+            device_id={"ctx": pair_z}, device_id_type=pl.DeviceIdType.MESH).start()
+
+    def arrived(owner, k, r):
+        push(owner, k, pt, 0, r).wait_recv()
+
+    def forward(owner, k, s, r):
+        push(owner, k, pt, s, r).start()
+
+    def own_out(k):
+        push(me, k, xn, 0, 2).start()
+        push(me, k, yn, 1, 4).start()
+
+    def from_sides(k):
+        arrived(rel_owner, k, rel_r)
+        push(rel_owner, k, rel_target, 3, 6).start()
+        if k in NEAR:
+            across(rel_owner, k, 7, rel_r)
+        forward(rel_owner, k, 4, 1 + rel_r)
+        arrived(oth_owner, k, oth_r)
+        if k in NEAR:
+            across(oth_owner, k, 8, oth_r)
+        forward(oth_owner, k, 5, 1 + oth_r)
+
+    def from_diag(k):
+        arrived(diag, k, 6)
+        if k in NEAR:
+            across(diag, k, 9, 6)
+        forward(diag, k, 6, 7)
+
+    def from_far(k):
+        arrived(rel_owner, k, rel_r)
+        forward(rel_owner, k, 4, 1 + rel_r)
+        arrived(oth_owner, k, oth_r)
+        forward(oth_owner, k, 5, 1 + oth_r)
+
+    locals_ = []
+    for g in range(GROUPS):
+        for section in range(3):
+            locals_.append(pltpu.make_async_copy(
+                qkv_in.at[:, pl.ds(section * heads_width + g * gw, gw)],
+                W.at[me, g, :, pl.ds(section * gw, gw)],
+                local_sem.at[3 * g + section]))
+    locals_.append(pltpu.make_async_copy(down_in, DT.at[me], local_sem.at[6]))
+    locals_.append(pltpu.make_async_copy(up_in, U.at[me], local_sem.at[7]))
+    locals_.append(pltpu.make_async_copy(out_in, O.at[me], local_sem.at[8]))
+    for copy in locals_:
+        copy.start()
     loads = []
     for t, (src, dst) in enumerate(((tokens_in, tokens), (outgrad_in, outgrad), (modulation_in, modulation))):
         load = pltpu.make_async_copy(src, dst, load_sem.at[t])
         load.start()
         loads.append(load)
+    for copy in locals_[:3]:
+        copy.wait()
     pl.semaphore_wait(barrier, ndp - 1 + nctx - 1)
-
-    parity = mz % 2
-    pair_z = mz + 1 - 2 * parity
-    big = (block // 16) * 5 // 24 * 16
-    rest = block - 4 * big
-    items, near = 8, 6
-
-    def view(ref, own, k):
-        if k == 2:
-            return out_in if own else O.at[ref]
-        if k == 3:
-            return down_in if own else DT.at[ref]
-        if k == 4:
-            return up_in if own else U.at[ref]
-        if k == 5:
-            span = pl.ds(0, rest)
-        elif k < 2:
-            span = pl.ds(pl.multiple_of(rest + (2 * parity + k) * big, 16), big)
-        else:
-            span = pl.ds(pl.multiple_of(rest + (2 * (1 - parity) + k - near) * big, 16), big)
-        return qkv_in.at[span, :] if own else W.at[ref, span, :]
-
-    def piece(owner, k):
-        return view(owner, False, k)
-
-    def own_piece(k):
-        return view(me, True, k)
-
-    def push(src, owner, k, target, s, r):
-        return pltpu.make_async_remote_copy(
-            src_ref=src, dst_ref=piece(owner, k), send_sem=gs_sem.at[s, k], recv_sem=gr_sem.at[r, k],
-            device_id={"dp": target}, device_id_type=pl.DeviceIdType.MESH)
-
-    def across(owner, k, s, r):
-        return pltpu.make_async_remote_copy(
-            src_ref=piece(owner, k), dst_ref=piece(owner, k), send_sem=gs_sem.at[s, k],
-            recv_sem=gr_sem.at[r, near + k],
-            device_id={"ctx": pair_z}, device_id_type=pl.DeviceIdType.MESH)
-
-    def arrived(owner, k, r):
-        push(piece(owner, k), owner, k, pt, 0, r).wait_recv()
-
-    def forward(owner, k, s, r):
-        push(piece(owner, k), owner, k, pt, s, r).start()
-
-    def own_out(k):
-        push(own_piece(k), me, k, xn, 0, 2).start()
-        push(own_piece(k), me, k, yn, 1, 4).start()
-
-    locals_ = []
-    for k in (0, 1, 2):
-        own_out(k)
-    for k in range(items):
-        copy = pltpu.make_async_copy(own_piece(k), piece(me, k), local_sem.at[k])
-        copy.start()
-        locals_.append(copy)
-        push(own_piece(k), me, k, pt, 2, 1).start()
+    own_out(NEAR[0])
+    for copy in locals_[3:]:
+        copy.wait()
+    own_out(DOWN)
+    own_out(UP)
+    own_out(REST[0])
+    for k in (0, 1, 2, 6, 7, 3, 4, 5) + OUT:
+        push(me, k, pt, 2, 1).start()
+    for load in loads:
+        load.wait()
 
     def cols(j):
         return pl.ds(pl.multiple_of(j * block, 128), block)
-
-    for load in loads:
-        load.wait()
 
     def sum_body(j, s):
         return s + jnp.sum(tokens[:, cols(j)].astype(F32), -1, keepdims=True)
@@ -430,71 +468,22 @@
 
     lax.fori_loop(0, ndp, norm_body, 0)
 
-    def from_sides(k):
-        arrived(rel_owner, k, rel_r)
-        push(piece(rel_owner, k), rel_owner, k, rel_target, 3, 6).start()
-        if k < 2:
-            across(rel_owner, k, 7, rel_r).start()
-        forward(rel_owner, k, 4, 1 + rel_r)
-        arrived(oth_owner, k, oth_r)
-        if k < 2:
-            across(oth_owner, k, 8, oth_r).start()
-        forward(oth_owner, k, 5, 1 + oth_r)
-
-    def from_diag(k):
-        arrived(diag, k, 6)
-        if k < 2:
-            across(diag, k, 9, 6).start()
-        forward(diag, k, 6, 7)
-
-    pt_owners = ((pt, 1), (place(y, x1, c1), 3), (place(y1, x, c1), 5))
-    last_owner = place(y1, x1, c1)
-
-    def grad_part(owner):
-        WT[...] += times_transposed(BG[owner], O[owner])
-
-    def qkv_part(owner):
-        RAW[...] += dot_nn(H[owner], W[owner])
+    far_side = place(y, x1, c1), place(y1, x, c1), place(y1, x1, c1)
+    pt_owners = ((pt, 1), (far_side[0], 3), (far_side[1], 5))
+    last_owner = far_side[2]
+
+    def grad_part(owner, g):
+        WT[g] += times_transposed(BG[owner], O[owner, g * gw : (g + 1) * gw, :])
+
+    def qkv_part(owner, g):
+        RAW[g] += dot_nn(H[owner], W[owner, g])
+
+    def low_part(owner):
         LOW[...] += times_transposed(H[owner], DT[owner])
 
-    RAW[...] = jnp.zeros_like(RAW)
-    LOW[...] = jnp.zeros_like(LOW)
-    WT[...] = jnp.zeros_like(WT)
-    for k in (0, 1):
-        from_sides(k)
-    for k in (3, 4, 5):
-        own_out(k)
-    for k in range(items):
-        locals_[k].wait()
-    grad_part(me)
-    qkv_part(me)
-    from_sides(2)
-    for k in (0, 1):
-        from_diag(k)
-    for k in (3, 4, 5):
-        from_sides(k)
-    from_diag(2)
-    for owner in (xn, yn):
-        grad_part(owner)
-    for owner, r in pt_owners:
-        arrived(owner, 2, r)
-        grad_part(owner)
-    grad_part(diag)
-    arrived(last_owner, 2, 7)
-    grad_part(last_owner)
-
-    def ctx_copy(src, dst, ssem, rsem, t):
-        return pltpu.make_async_remote_copy(
-            src_ref=src, dst_ref=dst, send_sem=ssem.at[t], recv_sem=rsem.at[t],
-            device_id={"ctx": lax.rem(mz + t, nctx)}, device_id_type=pl.DeviceIdType.MESH)
-
-    def exchange(sent, got, ssem, rsem):
-        copies = []
-        for t in range(1, nctx):
-            copy = ctx_copy(sent.at[lax.rem(mz + t, nctx)], got.at[mz], ssem, rsem, t)
-            copy.start()
-            copies.append(copy)
-        return copies
+    def got(owner, r, kinds):
+        for k in kinds:
+            arrived(owner, k, r)
 
     frames = rows // places
     across_rows = lax.broadcasted_iota(jnp.int32, (rows, rows), 0)
@@ -516,142 +505,291 @@
     def to_frame(value):
         return dot_nn(perm_back, value).astype(BF16)
 
-    DS[...] = to_place(WT[...].astype(BF16)).reshape(nctx, part, heads_width)
-    DR[mz] = DS[mz]
-    grad_copies = exchange(DS, DR, ds_sem, dr_sem)
-
-    for k in (near, near + 1):
-        arrived(rel_owner, k, rel_r)
-        forward(rel_owner, k, 4, 1 + rel_r)
-        arrived(oth_owner, k, oth_r)
-        forward(oth_owner, k, 5, 1 + oth_r)
-    for owner in (xn, yn):
-        qkv_part(owner)
-    for owner, r in pt_owners:
-        for k in range(items):
-            if k != 2:
-                arrived(owner, k, r)
-        qkv_part(owner)
-    for k in (3, 4, 5, near, near + 1):
-        from_diag(k)
-    qkv_part(diag)
-    for k in range(items):
-        if k != 2:
-            arrived(last_owner, k, 7)
-    qkv_part(last_owner)
-
-    up_rows = U[...].astype(F32).reshape(rank2, heads_width)
-    in_query = lax.broadcasted_iota(jnp.int32, (rank2, heads_width), 0) < rank2 // 2
-    up_query = jnp.where(in_query, up_rows, 0.0).astype(BF16)
-    up_value = jnp.where(in_query, 0.0, up_rows).astype(BF16)
-    low = LOW[...].astype(BF16)
-    RAW[:, :heads_width] += dot_nn(low, up_query)
-    RAW[:, 2 * heads_width :] += dot_nn(low, up_value)
-
-    def head(h, section=0):
-        lo = section * heads_width + h * HEAD_SIZE
+    def ctx_copy(src, dst, ssem, rsem, t):
+        return pltpu.make_async_remote_copy(
+            src_ref=src, dst_ref=dst, send_sem=ssem, recv_sem=rsem,
+            device_id={"ctx": lax.rem(mz + t, nctx)}, device_id_type=pl.DeviceIdType.MESH)
+
+    def exchange(sent, got_ref, ssem, rsem, g):
+        copies = []
+        got_ref[g, mz] = sent[g, mz]
+        for t in range(1, nctx):
+            copy = ctx_copy(
+                sent.at[g, lax.rem(mz + t, nctx)], got_ref.at[g, mz], ssem.at[g, t], rsem.at[g, t], t)
+            copy.start()
+            copies.append(copy)
+        return copies
+
+    def wait_all(copies):
+        for copy in copies:
+            copy.wait()
+
+    def lanes(i, section=0):
+        lo = section * gw + i * HEAD_SIZE
         return slice(lo, lo + HEAD_SIZE)
 
     def inverse_of(raw):
         return lax.rsqrt(jnp.mean(raw * raw, -1, keepdims=True) + EPSILON)
 
-    for section in range(3):
-        for h in range(nh):
-            raw = RAW[:, head(h, section)]
-            if section < 2:
-                raw = raw * inverse_of(raw)
-            QS[:, :, head(h, section)] = to_place(raw.astype(BF16)).reshape(nctx, part, HEAD_SIZE)
-    QR[mz] = QS[mz]
-    qkv_copies = exchange(QS, QR, qs_sem, qr_sem)
-    for copy in grad_copies:
-        copy.wait()
-    for copy in qkv_copies:
-        copy.wait()
+    def up_maps():
+        up_rows = U[...].astype(F32).reshape(rank2, heads_width)
+        in_query = lax.broadcasted_iota(jnp.int32, (rank2, heads_width), 0) < rank2 // 2
+        return (
+            jnp.where(in_query, up_rows, 0.0).astype(BF16),
+            jnp.where(in_query, 0.0, up_rows).astype(BF16),
+        )
+
+    def send_qkv(g):
+        up_query, up_value = up_maps()
+        low = LOW[...].astype(BF16)
+        mine = slice(g * gw, (g + 1) * gw)
+        RAW[g, :, :gw] += dot_nn(low, up_query[:, mine])
+        RAW[g, :, 2 * gw :] += dot_nn(low, up_value[:, mine])
+        for section in range(3):
+            for i in range(per_group):
+                raw = RAW[g, :, lanes(i, section)]
+                if section < 2:
+                    raw = raw * inverse_of(raw)
+                QS[g, :, :, lanes(i, section)] = to_place(raw.astype(BF16)).reshape(nctx, part, HEAD_SIZE)
+        return exchange(QS, QR, qs_sem, qr_sem, g)
+
+    def send_grad(h):
+        raw = WT[h // per_group, :, lanes(h % per_group)]
+        DS[h] = to_place(raw.astype(BF16)).reshape(nctx, part, HEAD_SIZE)
+        return exchange(DS, DR, ds_sem, dr_sem, h)
 
     scale = HEAD_SIZE ** (-0.5)
 
-    def whole(ref, where):
-        return ref[:, :, where].reshape(rows, HEAD_SIZE)
-
-    weights = []
-    for h in range(nh):
-        q, k = whole(QR, head(h)), whole(QR, head(h, 1))
-        v = whole(QR, head(h, 2))
-        expo = jnp.exp(times_transposed(q, k) * scale) * same
-        a = expo / jnp.sum(expo, -1, keepdims=True)
-        OS[:, :, head(h)] = dot_nn(a.astype(BF16), v).astype(BF16).reshape(nctx, part, HEAD_SIZE)
-        weights.append(a)
-    OR[mz] = OS[mz]
-    out_copies = exchange(OS, OR, os_sem, or_sem)
-    for h in range(nh):
-        q, k = whole(QR, head(h)), whole(QR, head(h, 1))
-        v, g = whole(QR, head(h, 2)), whole(DR, head(h))
-        a = weights[h]
-        dv = transposed_times(a.astype(BF16), g)
-        dp = times_transposed(g, v)
+    def whole(ref, g, where):
+        return ref[g, :, :, where].reshape(rows, HEAD_SIZE)
+
+    def attend_group(g):
+        for i in range(per_group):
+            q, k = whole(QR, g, lanes(i)), whole(QR, g, lanes(i, 1))
+            v = whole(QR, g, lanes(i, 2))
+            expo = jnp.exp(times_transposed(q, k) * scale) * same
+            a = expo / jnp.sum(expo, -1, keepdims=True)
+            OS[g, :, :, lanes(i)] = dot_nn(a.astype(BF16), v).astype(BF16).reshape(nctx, part, HEAD_SIZE)
+            AW[g * per_group + i] = a
+        return exchange(OS, OR, os_sem, or_sem, g)
+
+    def attend_back(h):
+        g, i = h // per_group, h % per_group
+        q, k = whole(QR, g, lanes(i)), whole(QR, g, lanes(i, 1))
+        v, d = whole(QR, g, lanes(i, 2)), whole(DR, h, slice(None))
+        a = AW[h]
+        dv = transposed_times(a.astype(BF16), d)
+        dp = times_transposed(d, v)
         ds = (a * (dp - jnp.sum(a * dp, -1, keepdims=True)) * scale).astype(BF16)
         dq = dot_nn(ds, k)
         dk = transposed_times(ds, q)
         for section, value in enumerate((dq, dk, dv)):
-            GS[:, :, head(h, section)] = value.astype(BF16).reshape(nctx, part, HEAD_SIZE)
-    GR[mz] = GS[mz]
-    back_copies = exchange(GS, GR, bs_sem, br_sem)
+            where = slice(section * HEAD_SIZE, (section + 1) * HEAD_SIZE)
+            GS[h, :, :, where] = value.astype(BF16).reshape(nctx, part, HEAD_SIZE)
+        return exchange(GS, GR, bs_sem, br_sem, h)
+
+    def norm_back(h):
+        g, i = h // per_group, h % per_group
+        for section in range(3):
+            where = lanes(i, section)
+            u = to_frame(whole(GR, h, slice(section * HEAD_SIZE, (section + 1) * HEAD_SIZE)))
+            if section < 2:
+                raw = RAW[g, :, where]
+                inv = inverse_of(raw)
+                uf = u.astype(F32)
+                inner = jnp.mean(raw * uf, -1, keepdims=True)
+                u = (inv * uf - raw * (inv * inv * inv) * inner).astype(BF16)
+            JG[g, :, where] = u
 
     grad_scale = total_tokens ** (-0.5)
-    for copy in out_copies:
-        copy.wait()
-    OS[...] = to_frame(OR[...].reshape(rows, heads_width)).reshape(nctx, part, heads_width)
+
+    def low_grad_part(g):
+        up_query, up_value = up_maps()
+        in_query = lax.broadcasted_iota(jnp.int32, (rank2, gw), 0) < rank2 // 2
+        mine = slice(g * gw, (g + 1) * gw)
+        jq, jv = JG[g, :, :gw], JG[g, :, 2 * gw :]
+        low = LT[...]
+        up_part = jnp.where(in_query, dot_nn(low, jq), dot_nn(low, jv)) * grad_scale
+        US[:, :, mine] = up_part.reshape(ndp, rank2 // ndp, gw).astype(BF16)
+        return times_transposed(jq, up_query[:, mine]) + times_transposed(jv, up_value[:, mine])
+
+    RAW[...] = jnp.zeros_like(RAW)
+    LOW[...] = jnp.zeros_like(LOW)
+    WT[...] = jnp.zeros_like(WT)
+    low_part(me)
+    for g in range(GROUPS):
+        qkv_part(me, g)
+        grad_part(me, g)
+
+    from_sides(NEAR[0])
+    from_sides(DOWN)
+    from_sides(UP)
+    from_sides(REST[0])
+    own_out(NEAR[1])
+    own_out(REST[1])
+    got(pt, 1, (0, 1, 2, DOWN, UP))
+    low_part(pt)
+    qkv_part(pt, 0)
+    from_diag(NEAR[0])
+    from_diag(DOWN)
+    from_diag(UP)
+    from_far(FAR[0])
+    from_diag(REST[0])
+    for owner in (xn, yn):
+        low_part(owner)
+        qkv_part(owner, 0)
+    low_part(diag)
+    for owner, r in pt_owners[1:]:
+        got(owner, r, (0, 1, 2, DOWN, UP))
+        low_part(owner)
+        qkv_part(owner, 0)
+    from_sides(NEAR[1])
+    from_diag(FAR[0])
+    qkv_part(diag, 0)
+    got(last_owner, 7, (0, 1, 2, DOWN, UP))
+    low_part(last_owner)
+    qkv_part(last_owner, 0)
+    qkv_copies = [send_qkv(0)]
+    LT[...] = LOW[...].T.astype(BF16)
+
+    from_sides(REST[1])
+    early, late = OUT[:per_group], OUT[per_group:]
+    for k in early:
+        own_out(k)
+    got(pt, 1, (3, 4, 5))
+    qkv_part(pt, 1)
+    from_diag(NEAR[1])
+    own_out(late[0])
+    from_far(FAR[1])
+    from_diag(REST[1])
+    for owner in (xn, yn):
+        qkv_part(owner, 1)
+    for k in early:
+        from_sides(k)
+    for k in late[1:]:
+        own_out(k)
+    wait_all(qkv_copies[0])
+    out_copies = [attend_group(0)]
+    for owner, r in pt_owners[1:]:
+        got(owner, r, (3, 4, 5))
+        qkv_part(owner, 1)
+    from_diag(FAR[1])
+    qkv_part(diag, 1)
+    from_sides(late[0])
+    got(last_owner, 7, (3, 4, 5))
+    qkv_part(last_owner, 1)
+    qkv_copies.append(send_qkv(1))
+
+    def start_grad(g, keys):
+        for owner in (xn, yn, diag):
+            grad_part(owner, g)
+        for owner, r in pt_owners:
+            got(owner, r, keys)
+            grad_part(owner, g)
+
+    def finish_grad(g, keys):
+        got(last_owner, 7, keys)
+        grad_part(last_owner, g)
+        return [send_grad(h) for h in range(g * per_group, (g + 1) * per_group)]
+
+    for k in early:
+        from_diag(k)
+    for k in late[1:]:
+        from_sides(k)
+    start_grad(0, early)
+    grad_copies = finish_grad(0, early)
+    for k in late:
+        from_diag(k)
+    start_grad(1, late)
+    grad_copies += finish_grad(1, late)
+    back_copies = []
+    for h in range(per_group):
+        wait_all(grad_copies[h])
+        back_copies.append(attend_back(h))
+    wait_all(qkv_copies[1])
+    out_copies.append(attend_group(1))
+    for h in range(per_group, nh):
+        wait_all(grad_copies[h])
+        back_copies.append(attend_back(h))
+
+    z_copies = []
+
+    def share(view, row):
+        for t in range(1, nctx):
+            copy = ctx_copy(view, view, zs_sem.at[row, t], zr_sem.at[row, t], t)
+            copy.start()
+            z_copies.append(copy)
+
+    for h in range(per_group):
+        wait_all(back_copies[h])
+        norm_back(h)
+
+    def first_hidden(j, _):
+        HG[j] = times_transposed(JG[0], W[j, 0])
+        return 0
+
+    lax.fori_loop(0, ndp, first_hidden, 0)
+    low_grad = low_grad_part(0)
+    for g in range(GROUPS):
+        wait_all(out_copies[g])
+        OF[:, g * gw : (g + 1) * gw] = to_frame(OR[g].reshape(rows, gw))
 
     def out_body(j, _):
-        branch = dot_nn(OS[...].reshape(rows, heads_width), O[j])
+        branch = dot_nn(OF[...], O[j])
         up = outgrad[:, cols(j)].astype(F32)
         mixed_out[:, cols(j)] = (
             tokens[:, cols(j)].astype(F32) + modulation[2, :, cols(j)] * branch
         ).astype(BF16)
-        ZM[mz, 2, pl.ds(j, 1), :] = jnp.sum(up * branch, 0, keepdims=True) * grad_scale
+        ZL[2, pl.ds(j, 1), :] = jnp.sum(up * branch, 0, keepdims=True) * grad_scale
         return 0
 
     lax.fori_loop(0, ndp, out_body, 0)
-
-    for copy in back_copies:
-        copy.wait()
-    for section in range(3):
-        for h in range(nh):
-            where = head(h, section)
-            u = to_frame(whole(GR, where))
-            if section < 2:
-                raw = RAW[:, where]
-                inv = inverse_of(raw)
-                uf = u.astype(F32)
-                inner = jnp.mean(raw * uf, -1, keepdims=True)
-                u = (inv * uf - raw * (inv * inv * inv) * inner).astype(BF16)
-            JG[:, where] = u
-    jq, jv = JG[:, :heads_width], JG[:, 2 * heads_width :]
-    LG[...] = (times_transposed(jq, up_query) + times_transposed(jv, up_value)).astype(BF16)
-    up_part = jnp.where(in_query, transposed_times(low, jq), transposed_times(low, jv)) * grad_scale
-    US[...] = up_part.reshape(ndp, rank2 // ndp, heads_width)
-
-    def down_body(j, _):
-        RS[j] = (transposed_times(LG[...], H[j]) * grad_scale).astype(BF16)
-        return 0
-
-    lax.fori_loop(0, ndp, down_body, 0)
-    reduce_copies = []
-    for t in range(1, ndp):
-        to = lax.rem(me + t, ndp)
-        for src, dst, ss, rs in ((RS, RR, rs_sem, rr_sem), (US, UR, us_sem, ur_sem)):
-            copy = pltpu.make_async_remote_copy(
-                src_ref=src.at[to], dst_ref=dst.at[t], send_sem=ss.at[t], recv_sem=rs.at[t],
-                device_id={"dp": to}, device_id_type=pl.DeviceIdType.MESH)
-            copy.start()
-            reduce_copies.append(copy)
+    ZM[mz, 2] = ZL[2].astype(BF16)
+    for h in range(per_group, nh):
+        wait_all(back_copies[h])
+        norm_back(h)
+    share(ZM.at[mz, 2], 0)
+    low_grad = low_grad + low_grad_part(1)
+    LG[...] = low_grad.astype(BF16)
+    LGT[...] = low_grad.T.astype(BF16)
+    half = rank2 // 2
+
+    def reduce_to(src, dst, ss, rs, to):
+        copy = pltpu.make_async_remote_copy(
+            src_ref=src, dst_ref=dst, send_sem=ss, recv_sem=rs,
+            device_id={"dp": to}, device_id_type=pl.DeviceIdType.MESH)
+        copy.start()
+        return copy
+
+    def others():
+        return [(t, lax.rem(me + t, ndp)) for t in range(1, ndp)]
+
+    up_copies = [
+        reduce_to(US.at[to], UR.at[t], us_sem.at[t], ur_sem.at[t], to) for t, to in others()
+    ]
+
+    def down_part(j):
+        both = (dot_nn(LGT[...], H[j]) * grad_scale).astype(BF16)
+        RS[j, 0] = both[:half]
+        RS[j, 1] = both[half:]
+
+    def reduce_down(i, t, to):
+        return reduce_to(RS.at[to, i], RR.at[t, i], rs_sem.at[i, t], rr_sem.at[i, t], to)
+
+    down_copies = [[], []]
+    for t, to in others():
+        down_part(to)
+        down_copies[0].append(reduce_down(0, t, to))
+    for t, to in others():
+        down_copies[1].append(reduce_down(1, t, to))
+    down_part(me)
 
     def hidden_body(j, sums):
         first, second = sums
-        hg = times_transposed(JG[...], W[j]) + dot_nn(LG[...], DT[j])
+        hg = HG[j] + times_transposed(JG[1], W[j, 1]) + dot_nn(LG[...], DT[j])
         n = N[j]
-        ZM[mz, 0, pl.ds(j, 1), :] = jnp.sum(hg, 0, keepdims=True) * grad_scale
-        ZM[mz, 1, pl.ds(j, 1), :] = jnp.sum(hg * n, 0, keepdims=True) * grad_scale
+        ZL[0, pl.ds(j, 1), :] = jnp.sum(hg, 0, keepdims=True) * grad_scale
+        ZL[1, pl.ds(j, 1), :] = jnp.sum(hg * n, 0, keepdims=True) * grad_scale
         ng = hg * (1.0 + modulation[1, :, cols(j)])
         HG[j] = ng
         return (
@@ -659,29 +797,26 @@
             second + jnp.sum(ng * n, -1, keepdims=True),
         )
 
+    def share_down(i):
+        wait_all(down_copies[i])
+        total = RS[me, i].astype(F32)
+        for t in range(1, ndp):
+            total = total + RR[t, i].astype(F32)
+        ZD[mz, i] = total.astype(BF16)
+        share(ZD.at[mz, i], 2 + i)
+
     zero = jnp.zeros((rows, 1), F32)
-    first, second = lax.fori_loop(0, ndp, hidden_body, (zero, zero))
-    z_copies = []
-
-    def share(ref, row):
-        for t in range(1, nctx):
-            copy = ctx_copy(ref.at[mz], ref.at[mz], zs_sem.at[row], zr_sem.at[row], t)
-            copy.start()
-            z_copies.append(copy)
-
-    share(ZM, 0)
-    for copy in reduce_copies:
-        copy.wait()
-    down_sum = RS[me].astype(F32)
-    up_sum = US[me]
+    sums = lax.fori_loop(0, ndp // 2, hidden_body, (zero, zero))
+    wait_all(up_copies)
+    up_sum = US[me].astype(F32)
     for t in range(1, ndp):
-        down_sum = down_sum + RR[t].astype(F32)
-        up_sum = up_sum + UR[t]
-    ZD[mz] = down_sum.astype(BF16)
-    ZU[mz] = up_sum
-    share(ZD, 1)
-    share(ZU, 2)
-
+        up_sum = up_sum + UR[t].astype(F32)
+    ZU[mz] = up_sum.astype(BF16)
+    share(ZU.at[mz], 1)
+    first, second = lax.fori_loop(ndp // 2, ndp, hidden_body, sums)
+    share_down(0)
+    ZM[mz, pl.ds(0, 2)] = ZL[0:2].astype(BF16)
+    share(ZM.at[mz, pl.ds(0, 2)], 4)
     first, second = first / width, second / width
 
     def last_body(j, _):
@@ -690,23 +825,24 @@
         return 0
 
     lax.fori_loop(0, ndp, last_body, 0)
-    for copy in z_copies:
-        copy.wait()
-    down_all, up_all, mod_all = ZD[0].astype(F32), ZU[0], ZM[0]
+    share_down(1)
+    wait_all(z_copies)
+    down_all, up_all, mod_all = ZD[0].astype(F32), ZU[0].astype(F32), ZM[0].astype(F32)
     for z in range(1, nctx):
         down_all = down_all + ZD[z].astype(F32)
-        up_all = up_all + ZU[z]
-        mod_all = mod_all + ZM[z]
-    down_out[...] = down_all
+        up_all = up_all + ZU[z].astype(F32)
+        mod_all = mod_all + ZM[z].astype(F32)
+    for i in range(2):
+        down_out[i * half : (i + 1) * half, :] = down_all[i]
     up_out[...] = up_all
     for j in range(ndp):
         for i in range(3):
             mod_out[i, :, j * block : (j + 1) * block] = mod_all[i, j : j + 1, :]
 
     for k in range(items):
-        used = range(10) if k < 2 else range(7) if k < near else (2, 4, 5, 6)
+        used = range(10) if k in NEAR else (2, 4, 5, 6) if k in FAR else range(7)
         for s in used:
-            push(piece(me, k), me, k, pt, s, 1).wait_send()
+            push(me, k, pt, s, 1).wait_send()
 
 
 def finish_kernel(*refs):
@@ -732,40 +868,47 @@
     hbm = pl.BlockSpec(memory_space=pltpu.HBM)
     sem = pltpu.SemaphoreType.DMA
     ur = rank2 // ndp
+    gw = hw // GROUPS
     scratch = [
         pltpu.VMEM((rows, width), BF16),
         pltpu.VMEM((3, 1, width), F32),
         pltpu.VMEM((rows, width), BF16),
-        pltpu.VMEM((ndp, block, 3 * hw), BF16),
+        pltpu.VMEM((ndp, GROUPS, block, 3 * gw), BF16),
         pltpu.VMEM((ndp, hw, block), BF16),
         pltpu.VMEM((ndp, rank2, block), BF16),
         pltpu.VMEM((ndp, ur, hw), BF16),
         pltpu.VMEM((ndp, rows, block), BF16),
         pltpu.VMEM((ndp, rows, block), F32),
         pltpu.VMEM((ndp, rows, block), BF16),
-        pltpu.VMEM((rows, 3 * hw), F32),
+        pltpu.VMEM((GROUPS, rows, 3 * gw), F32),
     ]
-    for w in (hw, 3 * hw, hw, 3 * hw):
-        scratch += [pltpu.VMEM((nctx, part, w), BF16)] * 2
+    nh = hw // HEAD_SIZE
+    for n, w in ((nh, HEAD_SIZE), (GROUPS, 3 * gw), (GROUPS, gw), (nh, 3 * HEAD_SIZE)):
+        scratch += [pltpu.VMEM((n, nctx, part, w), BF16)] * 2
     scratch += [
-        pltpu.VMEM((rows, hw), F32),
+        pltpu.VMEM((GROUPS, rows, gw), F32),
         pltpu.VMEM((rows, rank2), F32),
-        pltpu.VMEM((rows, 3 * hw), BF16),
+        pltpu.VMEM((rank2, rows), BF16),
+        pltpu.VMEM((GROUPS, rows, 3 * gw), BF16),
         pltpu.VMEM((rows, rank2), BF16),
+        pltpu.VMEM((rank2, rows), BF16),
         pltpu.VMEM((ndp, rows, block), F32),
-        pltpu.VMEM((ndp, rank2, block), BF16),
-        pltpu.VMEM((ndp, rank2, block), BF16),
-        pltpu.VMEM((ndp, ur, hw), F32),
-        pltpu.VMEM((ndp, ur, hw), F32),
-        pltpu.VMEM((nctx, rank2, block), BF16),
-        pltpu.VMEM((nctx, ur, hw), F32),
-        pltpu.VMEM((nctx, 3, ndp, block), F32),
+        pltpu.VMEM((nh, rows, rows), F32),
+        pltpu.VMEM((rows, hw), BF16),
+        pltpu.VMEM((ndp, 2, rank2 // 2, block), BF16),
+        pltpu.VMEM((ndp, 2, rank2 // 2, block), BF16),
+        pltpu.VMEM((ndp, ur, hw), BF16),
+        pltpu.VMEM((ndp, ur, hw), BF16),
+        pltpu.VMEM((nctx, 2, rank2 // 2, block), BF16),
+        pltpu.VMEM((nctx, ur, hw), BF16),
+        pltpu.VMEM((nctx, 3, ndp, block), BF16),
+        pltpu.VMEM((3, ndp, block), F32),
         sem((3,)),
-        sem((8,)),
-        sem((10, 8)),
-        sem((8, 8)),
+        sem((9,)),
+        sem((10, 8 + nh)),
+        sem((8, 8 + nh)),
     ]
-    scratch += [sem((nctx,))] * 8 + [sem((ndp,))] * 4 + [sem((3, nctx))] * 2
+    scratch += [sem((nh, nctx))] * 8 + [sem((2, ndp))] * 2 + [sem((ndp,))] * 2 + [sem((5, nctx))] * 2
     results = pl.pallas_call(
         functools.partial(layer_kernel, dims),
         out_shape=(

time: 93.2 us -> 84.2 us (0.903)
  Pallas kernels: 92.4 us -> 83.4 us
    pallas_call x1, Pallas kernels: 91.2 us -> 82.2 us  [per_device_kernel(): pl.pallas_call(functools.partial(layer_kernel, dims), out_shape=(pltpu.VM...]
where the time goes in v2:
time: 84.2 us; the launch traced here: 84.1 us
  Pallas kernels  83.4 us (99%)
    pallas_call x1, Pallas kernels, per_device_kernel(): pl.pallas_call(functools.partial(layer_kernel, dims), out_shape=(pltpu.VM...  82.2 us

profile of v2, /device:TPU:0, one launch (start us, length us, event | category | flops | bytes accessed | tf_op | source)
XLA Modules:
  0.0 84.1 jit_solution(3304120426652564977)
XLA Ops:
  0.6 82.2 %shard_map.110 = (bf16[128,3072]{1,0:T(8,128)(2,1)S(1)}, bf16[128,3072]{1,0:T(8,128)(2,1)S(1)}, f32[3,1,3072]{2,1,0:T(1,128)S(1)}, f32[64,384]{1,0:T(8,128)S(1)}, f32[8,512]{1,0:T(8,128)S(1)}) custom-call(bf16[128,3072]{1,0:T(8,128)(2,1)} %bitcast.8, f32[3,1,3072]{2,1,0:T(1,128)} %bitcast.11, bf16[128,3072]{1,0:T(8,128)(2,1)} %bitcast.9, ...), custom_call_target="tpu_custom_call" | custom-call | tf_op jit(solution)/shard_map/pallas_call | solution.py:912
  82.8 1.2 %shard_map.111 = (bf16[128,3072]{1,0:T(8,128)(2,1)}, bf16[128,3072]{1,0:T(8,128)(2,1)}, f32[3,1,3072]{2,1,0:T(1,128)}, f32[64,384]{1,0:T(8,128)}, f32[8,512]{1,0:T(8,128)}) custom-call(bf16[128,3072]{1,0:T(8,128)(2,1)S(1)} %get-tuple-element.15.refs_0_, bf16[128,3072]{1,0:T(8,128)(2,1)S(1)} %get-tuple-element.16.refs_1_, ...), custom_call_target="tpu_custom_call" | custom-call | tf_op jit(solution)/shard_map/pallas_call | solution.py:936

commit v3 on v2

--- a/solution.py
+++ b/solution.py
@@ -305,7 +305,6 @@
     return lax.dot_general(a, b, (((1,), (0,)), ((), ())), preferred_element_type=F32)
 
 
-GROUPS = 2
 SHARED_ROWS = 16
 
 
@@ -325,8 +324,7 @@
     ndp, nctx, rows, places, width, block, heads_width, rank2, total_tokens = dims
     nh = heads_width // HEAD_SIZE
     part = rows // nctx
-    gw = heads_width // GROUPS
-    per_group = nh // GROUPS
+    head_width = 3 * HEAD_SIZE
     me = lax.axis_index("dp")
     mz = lax.axis_index("ctx")
     y, x, c = me // 4, (me // 2) % 2, me % 2
@@ -349,10 +347,13 @@
     pair_z = mz + 1 - 2 * parity
     big = block // 48 * SHARED_ROWS
     rest = block - 2 * big
-    NEAR, REST, FAR = (0, 3), (1, 4), (2, 5)
-    DOWN, UP = 6, 7
-    OUT = tuple(range(8, 8 + nh))
-    items = 8 + nh
+    NEAR, REST, FAR = (tuple(range(i, 3 * nh, 3)) for i in range(3))
+    DOWN, UP = 3 * nh, 3 * nh + 1
+    OUT = tuple(range(3 * nh + 2, 4 * nh + 2))
+    items = 4 * nh + 2
+
+    def place_of(h):
+        return h // 2, h % 2 * head_width
 
     def piece(owner, k):
         if k in OUT:
@@ -366,7 +367,8 @@
         else:
             side = parity if k in NEAR else 1 - parity
             span = pl.ds(pl.multiple_of(rest + side * big, 16), big)
-        return W.at[owner, k // 3, span, :]
+        pair, lo = place_of(k // 3)
+        return W.at[owner, pair, span, pl.ds(lo, head_width)]
 
     def push(owner, k, target, s, r):
         return pltpu.make_async_remote_copy(
@@ -414,15 +416,15 @@
         forward(oth_owner, k, 5, 1 + oth_r)
 
     locals_ = []
-    for g in range(GROUPS):
+    for h in range(nh):
+        pair, lo = place_of(h)
         for section in range(3):
             locals_.append(pltpu.make_async_copy(
-                qkv_in.at[:, pl.ds(section * heads_width + g * gw, gw)],
-                W.at[me, g, :, pl.ds(section * gw, gw)],
-                local_sem.at[3 * g + section]))
-    locals_.append(pltpu.make_async_copy(down_in, DT.at[me], local_sem.at[6]))
-    locals_.append(pltpu.make_async_copy(up_in, U.at[me], local_sem.at[7]))
-    locals_.append(pltpu.make_async_copy(out_in, O.at[me], local_sem.at[8]))
+                qkv_in.at[:, pl.ds(section * heads_width + h * HEAD_SIZE, HEAD_SIZE)],
+                W.at[me, pair, :, pl.ds(lo + section * HEAD_SIZE, HEAD_SIZE)],
+                local_sem.at[3 * h + section]))
+    for t, (src, dst) in enumerate(((down_in, DT), (up_in, U), (out_in, O))):
+        locals_.append(pltpu.make_async_copy(src, dst.at[me], local_sem.at[3 * nh + t]))
     for copy in locals_:
         copy.start()
     loads = []
@@ -433,13 +435,11 @@
     for copy in locals_[:3]:
         copy.wait()
     pl.semaphore_wait(barrier, ndp - 1 + nctx - 1)
-    own_out(NEAR[0])
     for copy in locals_[3:]:
         copy.wait()
-    own_out(DOWN)
-    own_out(UP)
-    own_out(REST[0])
-    for k in (0, 1, 2, 6, 7, 3, 4, 5) + OUT:
+    own_out(NEAR[0])
+    own_out(NEAR[2])
+    for k in (0, 1, 2, DOWN, UP) + tuple(range(3, 3 * nh)) + OUT:
         push(me, k, pt, 2, 1).start()
     for load in loads:
         load.wait()
@@ -472,11 +472,12 @@
     pt_owners = ((pt, 1), (far_side[0], 3), (far_side[1], 5))
     last_owner = far_side[2]
 
-    def grad_part(owner, g):
-        WT[g] += times_transposed(BG[owner], O[owner, g * gw : (g + 1) * gw, :])
-
-    def qkv_part(owner, g):
-        RAW[g] += dot_nn(H[owner], W[owner, g])
+    def grad_part(owner, h):
+        WT[h] += times_transposed(BG[owner], O[owner, h * HEAD_SIZE : (h + 1) * HEAD_SIZE, :])
+
+    def qkv_part(owner, h):
+        pair, lo = place_of(h)
+        RAW[h] += dot_nn(H[owner], W[owner, pair, :, lo : lo + head_width])
 
     def low_part(owner):
         LOW[...] += times_transposed(H[owner], DT[owner])
@@ -524,9 +525,8 @@
         for copy in copies:
             copy.wait()
 
-    def lanes(i, section=0):
-        lo = section * gw + i * HEAD_SIZE
-        return slice(lo, lo + HEAD_SIZE)
+    def lanes(section):
+        return slice(section * HEAD_SIZE, (section + 1) * HEAD_SIZE)
 
     def inverse_of(raw):
         return lax.rsqrt(jnp.mean(raw * raw, -1, keepdims=True) + EPSILON)
@@ -539,44 +539,39 @@
             jnp.where(in_query, 0.0, up_rows).astype(BF16),
         )
 
-    def send_qkv(g):
+    def send_qkv(h):
         up_query, up_value = up_maps()
         low = LOW[...].astype(BF16)
-        mine = slice(g * gw, (g + 1) * gw)
-        RAW[g, :, :gw] += dot_nn(low, up_query[:, mine])
-        RAW[g, :, 2 * gw :] += dot_nn(low, up_value[:, mine])
+        mine = lanes(h)
+        RAW[h, :, lanes(0)] += dot_nn(low, up_query[:, mine])
+        RAW[h, :, lanes(2)] += dot_nn(low, up_value[:, mine])
         for section in range(3):
-            for i in range(per_group):
-                raw = RAW[g, :, lanes(i, section)]
-                if section < 2:
-                    raw = raw * inverse_of(raw)
-                QS[g, :, :, lanes(i, section)] = to_place(raw.astype(BF16)).reshape(nctx, part, HEAD_SIZE)
-        return exchange(QS, QR, qs_sem, qr_sem, g)
+            raw = RAW[h, :, lanes(section)]
+            if section < 2:
+                raw = raw * inverse_of(raw)
+            QS[h, :, :, lanes(section)] = to_place(raw.astype(BF16)).reshape(nctx, part, HEAD_SIZE)
+        return exchange(QS, QR, qs_sem, qr_sem, h)
 
     def send_grad(h):
-        raw = WT[h // per_group, :, lanes(h % per_group)]
-        DS[h] = to_place(raw.astype(BF16)).reshape(nctx, part, HEAD_SIZE)
+        DS[h] = to_place(WT[h].astype(BF16)).reshape(nctx, part, HEAD_SIZE)
         return exchange(DS, DR, ds_sem, dr_sem, h)
 
     scale = HEAD_SIZE ** (-0.5)
 
-    def whole(ref, g, where):
-        return ref[g, :, :, where].reshape(rows, HEAD_SIZE)
-
-    def attend_group(g):
-        for i in range(per_group):
-            q, k = whole(QR, g, lanes(i)), whole(QR, g, lanes(i, 1))
-            v = whole(QR, g, lanes(i, 2))
-            expo = jnp.exp(times_transposed(q, k) * scale) * same
-            a = expo / jnp.sum(expo, -1, keepdims=True)
-            OS[g, :, :, lanes(i)] = dot_nn(a.astype(BF16), v).astype(BF16).reshape(nctx, part, HEAD_SIZE)
-            AW[g * per_group + i] = a
-        return exchange(OS, OR, os_sem, or_sem, g)
+    def whole(ref, h, section=0):
+        return ref[h, :, :, lanes(section)].reshape(rows, HEAD_SIZE)
+
+    def attend(h):
+        q, k, v = (whole(QR, h, section) for section in range(3))
+        expo = jnp.exp(times_transposed(q, k) * scale) * same
+        a = expo / jnp.sum(expo, -1, keepdims=True)
+        OS[h] = dot_nn(a.astype(BF16), v).astype(BF16).reshape(nctx, part, HEAD_SIZE)
+        AW[h] = a
+        return exchange(OS, OR, os_sem, or_sem, h)
 
     def attend_back(h):
-        g, i = h // per_group, h % per_group
-        q, k = whole(QR, g, lanes(i)), whole(QR, g, lanes(i, 1))
-        v, d = whole(QR, g, lanes(i, 2)), whole(DR, h, slice(None))
+        q, k, v = (whole(QR, h, section) for section in range(3))
+        d = whole(DR, h)
         a = AW[h]
         dv = transposed_times(a.astype(BF16), d)
         dp = times_transposed(d, v)
@@ -584,155 +579,96 @@
         dq = dot_nn(ds, k)
         dk = transposed_times(ds, q)
         for section, value in enumerate((dq, dk, dv)):
-            where = slice(section * HEAD_SIZE, (section + 1) * HEAD_SIZE)
-            GS[h, :, :, where] = value.astype(BF16).reshape(nctx, part, HEAD_SIZE)
+            GS[h, :, :, lanes(section)] = value.astype(BF16).reshape(nctx, part, HEAD_SIZE)
         return exchange(GS, GR, bs_sem, br_sem, h)
 
     def norm_back(h):
-        g, i = h // per_group, h % per_group
+        pair, lo = place_of(h)
         for section in range(3):
-            where = lanes(i, section)
-            u = to_frame(whole(GR, h, slice(section * HEAD_SIZE, (section + 1) * HEAD_SIZE)))
+            u = to_frame(whole(GR, h, section))
             if section < 2:
-                raw = RAW[g, :, where]
+                raw = RAW[h, :, lanes(section)]
                 inv = inverse_of(raw)
                 uf = u.astype(F32)
                 inner = jnp.mean(raw * uf, -1, keepdims=True)
                 u = (inv * uf - raw * (inv * inv * inv) * inner).astype(BF16)
-            JG[g, :, where] = u
+            JG[pair, :, lo + section * HEAD_SIZE : lo + (section + 1) * HEAD_SIZE] = u
 
     grad_scale = total_tokens ** (-0.5)
 
-    def low_grad_part(g):
+    def low_grad_part(h):
         up_query, up_value = up_maps()
-        in_query = lax.broadcasted_iota(jnp.int32, (rank2, gw), 0) < rank2 // 2
-        mine = slice(g * gw, (g + 1) * gw)
-        jq, jv = JG[g, :, :gw], JG[g, :, 2 * gw :]
+        in_query = lax.broadcasted_iota(jnp.int32, (rank2, HEAD_SIZE), 0) < rank2 // 2
+        mine = lanes(h)
+        pair, lo = place_of(h)
+        jq = JG[pair, :, lo : lo + HEAD_SIZE]
+        jv = JG[pair, :, lo + 2 * HEAD_SIZE : lo + head_width]
         low = LT[...]
         up_part = jnp.where(in_query, dot_nn(low, jq), dot_nn(low, jv)) * grad_scale
-        US[:, :, mine] = up_part.reshape(ndp, rank2 // ndp, gw).astype(BF16)
+        US[:, :, mine] = up_part.reshape(ndp, rank2 // ndp, HEAD_SIZE).astype(BF16)
         return times_transposed(jq, up_query[:, mine]) + times_transposed(jv, up_value[:, mine])
 
     RAW[...] = jnp.zeros_like(RAW)
     LOW[...] = jnp.zeros_like(LOW)
     WT[...] = jnp.zeros_like(WT)
     low_part(me)
-    for g in range(GROUPS):
-        qkv_part(me, g)
-        grad_part(me, g)
-
-    from_sides(NEAR[0])
-    from_sides(DOWN)
-    from_sides(UP)
-    from_sides(REST[0])
-    own_out(NEAR[1])
-    own_out(REST[1])
-    got(pt, 1, (0, 1, 2, DOWN, UP))
-    low_part(pt)
-    qkv_part(pt, 0)
-    from_diag(NEAR[0])
-    from_diag(DOWN)
-    from_diag(UP)
-    from_far(FAR[0])
-    from_diag(REST[0])
-    for owner in (xn, yn):
-        low_part(owner)
-        qkv_part(owner, 0)
-    low_part(diag)
-    for owner, r in pt_owners[1:]:
-        got(owner, r, (0, 1, 2, DOWN, UP))
-        low_part(owner)
-        qkv_part(owner, 0)
-    from_sides(NEAR[1])
-    from_diag(FAR[0])
-    qkv_part(diag, 0)
-    got(last_owner, 7, (0, 1, 2, DOWN, UP))
-    low_part(last_owner)
-    qkv_part(last_owner, 0)
-    qkv_copies = [send_qkv(0)]
-    LT[...] = LOW[...].T.astype(BF16)
-
-    from_sides(REST[1])
-    early, late = OUT[:per_group], OUT[per_group:]
-    for k in early:
-        own_out(k)
-    got(pt, 1, (3, 4, 5))
-    qkv_part(pt, 1)
-    from_diag(NEAR[1])
-    own_out(late[0])
-    from_far(FAR[1])
-    from_diag(REST[1])
-    for owner in (xn, yn):
-        qkv_part(owner, 1)
-    for k in early:
-        from_sides(k)
-    for k in late[1:]:
-        own_out(k)
-    wait_all(qkv_copies[0])
-    out_copies = [attend_group(0)]
-    for owner, r in pt_owners[1:]:
-        got(owner, r, (3, 4, 5))
-        qkv_part(owner, 1)
-    from_diag(FAR[1])
-    qkv_part(diag, 1)
-    from_sides(late[0])
-    got(last_owner, 7, (3, 4, 5))
-    qkv_part(last_owner, 1)
-    qkv_copies.append(send_qkv(1))
-
-    def start_grad(g, keys):
+    for h in range(nh):
+        qkv_part(me, h)
+        grad_part(me, h)
+
+    def kinds(h):
+        return (NEAR[h], REST[h], FAR[h])
+
+    qkv_copies, out_copies, grad_copies, back_copies = {}, {}, {}, {}
+    low_taken = set()
+
+    def take(name, owner, h, r=None):
+        if r is not None:
+            got(owner, r, kinds(h))
+        if name not in low_taken:
+            low_taken.add(name)
+            if r is not None:
+                got(owner, r, (DOWN, UP))
+            low_part(owner)
+        qkv_part(owner, h)
+
+    def qkv_middle(h):
+        take(0, pt, h, 1)
+        take(1, xn, h)
+        take(2, yn, h)
+        for i, (owner, r) in enumerate(pt_owners[1:]):
+            take(3 + i, owner, h, r)
+
+    def qkv_end(h):
+        take(5, diag, h)
+        take(6, last_owner, h, 7)
+        if len(qkv_copies) == 0:
+            LT[...] = LOW[...].T.astype(BF16)
+        qkv_copies[h] = send_qkv(h)
+
+    def grad_start(h):
         for owner in (xn, yn, diag):
-            grad_part(owner, g)
+            grad_part(owner, h)
         for owner, r in pt_owners:
-            got(owner, r, keys)
-            grad_part(owner, g)
-
-    def finish_grad(g, keys):
-        got(last_owner, 7, keys)
-        grad_part(last_owner, g)
-        return [send_grad(h) for h in range(g * per_group, (g + 1) * per_group)]
-
-    for k in early:
-        from_diag(k)
-    for k in late[1:]:
-        from_sides(k)
-    start_grad(0, early)
-    grad_copies = finish_grad(0, early)
-    for k in late:
-        from_diag(k)
-    start_grad(1, late)
-    grad_copies += finish_grad(1, late)
-    back_copies = []
-    for h in range(per_group):
+            arrived(owner, OUT[h], r)
+            grad_part(owner, h)
+
+    def grad_end(h):
+        arrived(last_owner, OUT[h], 7)
+        grad_part(last_owner, h)
+        grad_copies[h] = send_grad(h)
+
+    def attend_step(h):
+        wait_all(qkv_copies[h])
+        out_copies[h] = attend(h)
+
+    def back_step(h):
         wait_all(grad_copies[h])
-        back_copies.append(attend_back(h))
-    wait_all(qkv_copies[1])
-    out_copies.append(attend_group(1))
-    for h in range(per_group, nh):
-        wait_all(grad_copies[h])
-        back_copies.append(attend_back(h))
-
-    z_copies = []
-
-    def share(view, row):
-        for t in range(1, nctx):
-            copy = ctx_copy(view, view, zs_sem.at[row, t], zr_sem.at[row, t], t)
-            copy.start()
-            z_copies.append(copy)
-
-    for h in range(per_group):
-        wait_all(back_copies[h])
-        norm_back(h)
+        back_copies[h] = attend_back(h)
 
     def first_hidden(j, _):
         HG[j] = times_transposed(JG[0], W[j, 0])
         return 0
-
-    lax.fori_loop(0, ndp, first_hidden, 0)
-    low_grad = low_grad_part(0)
-    for g in range(GROUPS):
-        wait_all(out_copies[g])
-        OF[:, g * gw : (g + 1) * gw] = to_frame(OR[g].reshape(rows, gw))
 
     def out_body(j, _):
         branch = dot_nn(OF[...], O[j])
@@ -743,13 +679,103 @@
         ZL[2, pl.ds(j, 1), :] = jnp.sum(up * branch, 0, keepdims=True) * grad_scale
         return 0
 
+    from_sides(NEAR[0])
+    own_out(NEAR[1])
+    own_out(UP)
+    own_out(DOWN)
+    own_out(REST[1])
+    from_sides(NEAR[2])
+    from_diag(NEAR[0])
+    own_out(REST[0])
+    from_sides(NEAR[1])
+    from_sides(DOWN)
+    from_far(FAR[0])
+    own_out(REST[2])
+    from_diag(NEAR[2])
+    from_sides(UP)
+    from_far(FAR[2])
+    from_sides(REST[0])
+    from_diag(FAR[0])
+    own_out(NEAR[3])
+    from_diag(NEAR[1])
+    from_sides(REST[2])
+    from_sides(REST[1])
+    from_sides(NEAR[3])
+    qkv_middle(0)
+    own_out(OUT[0])
+    from_far(FAR[1])
+    own_out(REST[3])
+    from_diag(UP)
+    own_out(OUT[1])
+    from_diag(DOWN)
+    from_diag(REST[0])
+    qkv_middle(1)
+    from_diag(REST[1])
+    from_diag(FAR[2])
+    from_diag(REST[2])
+    qkv_end(0)
+    from_diag(FAR[1])
+    qkv_end(1)
+    from_diag(NEAR[3])
+    qkv_middle(2)
+    from_sides(OUT[0])
+    qkv_end(2)
+    from_far(FAR[3])
+    attend_step(0)
+    from_sides(REST[3])
+    from_sides(OUT[1])
+    attend_step(1)
+    from_diag(OUT[0])
+    own_out(OUT[3])
+    grad_start(0)
+    from_diag(REST[3])
+    from_diag(FAR[3])
+    own_out(OUT[2])
+    grad_end(0)
+    qkv_middle(3)
+    from_diag(OUT[1])
+    grad_start(1)
+    qkv_end(3)
+    from_sides(OUT[3])
+    grad_end(1)
+    attend_step(2)
+    from_sides(OUT[2])
+    back_step(0)
+    from_diag(OUT[3])
+    grad_start(3)
+    grad_end(3)
+    attend_step(3)
+    from_diag(OUT[2])
+    back_step(1)
+    grad_start(2)
+    grad_end(2)
+    back_step(3)
+    for h in range(nh):
+        wait_all(out_copies[h])
+        OF[:, lanes(h)] = to_frame(whole(OR, h))
+
     lax.fori_loop(0, ndp, out_body, 0)
+    back_step(2)
+    for h in range(2):
+        wait_all(back_copies[h])
+        norm_back(h)
+    lax.fori_loop(0, ndp, first_hidden, 0)
+    low_grad = low_grad_part(0) + low_grad_part(1)
+    z_copies = []
+
+    def share(view, row):
+        for t in range(1, nctx):
+            copy = ctx_copy(view, view, zs_sem.at[row, t], zr_sem.at[row, t], t)
+            copy.start()
+            z_copies.append(copy)
+
     ZM[mz, 2] = ZL[2].astype(BF16)
-    for h in range(per_group, nh):
+    for h in range(2, nh):
         wait_all(back_copies[h])
         norm_back(h)
     share(ZM.at[mz, 2], 0)
-    low_grad = low_grad + low_grad_part(1)
+    for h in range(2, nh):
+        low_grad = low_grad + low_grad_part(h)
     LG[...] = low_grad.astype(BF16)
     LGT[...] = low_grad.T.astype(BF16)
     half = rank2 // 2
@@ -806,14 +832,13 @@
         share(ZD.at[mz, i], 2 + i)
 
     zero = jnp.zeros((rows, 1), F32)
-    sums = lax.fori_loop(0, ndp // 2, hidden_body, (zero, zero))
+    first, second = lax.fori_loop(0, ndp, hidden_body, (zero, zero))
     wait_all(up_copies)
     up_sum = US[me].astype(F32)
     for t in range(1, ndp):
         up_sum = up_sum + UR[t].astype(F32)
     ZU[mz] = up_sum.astype(BF16)
     share(ZU.at[mz], 1)
-    first, second = lax.fori_loop(ndp // 2, ndp, hidden_body, sums)
     share_down(0)
     ZM[mz, pl.ds(0, 2)] = ZL[0:2].astype(BF16)
     share(ZM.at[mz, pl.ds(0, 2)], 4)
@@ -868,28 +893,28 @@
     hbm = pl.BlockSpec(memory_space=pltpu.HBM)
     sem = pltpu.SemaphoreType.DMA
     ur = rank2 // ndp
-    gw = hw // GROUPS
+    nh = hw // HEAD_SIZE
+    three = 3 * HEAD_SIZE
     scratch = [
         pltpu.VMEM((rows, width), BF16),
         pltpu.VMEM((3, 1, width), F32),
         pltpu.VMEM((rows, width), BF16),
-        pltpu.VMEM((ndp, GROUPS, block, 3 * gw), BF16),
+        pltpu.VMEM((ndp, nh // 2, block, 2 * three), BF16),
         pltpu.VMEM((ndp, hw, block), BF16),
         pltpu.VMEM((ndp, rank2, block), BF16),
         pltpu.VMEM((ndp, ur, hw), BF16),
         pltpu.VMEM((ndp, rows, block), BF16),
         pltpu.VMEM((ndp, rows, block), F32),
         pltpu.VMEM((ndp, rows, block), BF16),
-        pltpu.VMEM((GROUPS, rows, 3 * gw), F32),
+        pltpu.VMEM((nh, rows, three), F32),
     ]
-    nh = hw // HEAD_SIZE
-    for n, w in ((nh, HEAD_SIZE), (GROUPS, 3 * gw), (GROUPS, gw), (nh, 3 * HEAD_SIZE)):
-        scratch += [pltpu.VMEM((n, nctx, part, w), BF16)] * 2
+    for w in (HEAD_SIZE, three, HEAD_SIZE, three):
+        scratch += [pltpu.VMEM((nh, nctx, part, w), BF16)] * 2
     scratch += [
-        pltpu.VMEM((GROUPS, rows, gw), F32),
+        pltpu.VMEM((nh, rows, HEAD_SIZE), F32),
         pltpu.VMEM((rows, rank2), F32),
         pltpu.VMEM((rank2, rows), BF16),
-        pltpu.VMEM((GROUPS, rows, 3 * gw), BF16),
+        pltpu.VMEM((nh // 2, rows, 2 * three), BF16),
         pltpu.VMEM((rows, rank2), BF16),
         pltpu.VMEM((rank2, rows), BF16),
         pltpu.VMEM((ndp, rows, block), F32),
@@ -904,9 +929,9 @@
         pltpu.VMEM((nctx, 3, ndp, block), BF16),
         pltpu.VMEM((3, ndp, block), F32),
         sem((3,)),
-        sem((9,)),
-        sem((10, 8 + nh)),
-        sem((8, 8 + nh)),
+        sem((3 * nh + 3,)),
+        sem((10, 4 * nh + 2)),
+        sem((8, 4 * nh + 2)),
     ]
     scratch += [sem((nh, nctx))] * 8 + [sem((2, ndp))] * 2 + [sem((ndp,))] * 2 + [sem((5, nctx))] * 2
     results = pl.pallas_call(

time: 84.2 us -> 81.5 us (0.968)
  Pallas kernels: 83.4 us -> 80.7 us
    pallas_call x1, Pallas kernels: 82.2 us -> 79.5 us  [per_device_kernel(): pl.pallas_call(functools.partial(layer_kernel, dims), out_shape=(pltpu.VM...]
where the time goes in v3:
time: 81.5 us; the launch traced here: 81.3 us
  Pallas kernels  80.7 us (99%)
    pallas_call x1, Pallas kernels, per_device_kernel(): pl.pallas_call(functools.partial(layer_kernel, dims), out_shape=(pltpu.VM...  79.5 us

profile of v3, /device:TPU:0, one launch (start us, length us, event | category | flops | bytes accessed | tf_op | source)
XLA Modules:
  0.0 81.3 jit_solution(9300016680194569270)
XLA Ops:
  0.6 79.5 %shard_map.110 = (bf16[128,3072]{1,0:T(8,128)(2,1)S(1)}, bf16[128,3072]{1,0:T(8,128)(2,1)S(1)}, f32[3,1,3072]{2,1,0:T(1,128)S(1)}, f32[64,384]{1,0:T(8,128)S(1)}, f32[8,512]{1,0:T(8,128)S(1)}) custom-call(bf16[128,3072]{1,0:T(8,128)(2,1)} %bitcast.8, f32[3,1,3072]{2,1,0:T(1,128)} %bitcast.11, bf16[128,3072]{1,0:T(8,128)(2,1)} %bitcast.9, ...), custom_call_target="tpu_custom_call" | custom-call | tf_op jit(solution)/shard_map/pallas_call | solution.py:937
  80.1 1.2 %shard_map.111 = (bf16[128,3072]{1,0:T(8,128)(2,1)}, bf16[128,3072]{1,0:T(8,128)(2,1)}, f32[3,1,3072]{2,1,0:T(1,128)}, f32[64,384]{1,0:T(8,128)}, f32[8,512]{1,0:T(8,128)}) custom-call(bf16[128,3072]{1,0:T(8,128)(2,1)S(1)} %get-tuple-element.15.refs_0_, bf16[128,3072]{1,0:T(8,128)(2,1)S(1)} %get-tuple-element.16.refs_1_, ...), custom_call_target="tpu_custom_call" | custom-call | tf_op jit(solution)/shard_map/pallas_call | solution.py:961

commit v4 on v3

--- a/solution.py
+++ b/solution.py
@@ -435,9 +435,9 @@
     for copy in locals_[:3]:
         copy.wait()
     pl.semaphore_wait(barrier, ndp - 1 + nctx - 1)
+    own_out(NEAR[0])
     for copy in locals_[3:]:
         copy.wait()
-    own_out(NEAR[0])
     own_out(NEAR[2])
     for k in (0, 1, 2, DOWN, UP) + tuple(range(3, 3 * nh)) + OUT:
         push(me, k, pt, 2, 1).start()
@@ -746,9 +746,9 @@
     grad_end(3)
     attend_step(3)
     from_diag(OUT[2])
-    back_step(1)
     grad_start(2)
     grad_end(2)
+    back_step(1)
     back_step(3)
     for h in range(nh):
         wait_all(out_copies[h])
@@ -769,11 +769,13 @@
             copy.start()
             z_copies.append(copy)
 
-    ZM[mz, 2] = ZL[2].astype(BF16)
+    for i in range(2):
+        ZM[i, mz, 2] = ZL[2, i * (ndp // 2) : (i + 1) * (ndp // 2)].astype(BF16)
     for h in range(2, nh):
         wait_all(back_copies[h])
         norm_back(h)
-    share(ZM.at[mz, 2], 0)
+    for i in range(2):
+        share(ZM.at[i, mz, 2], i)
     for h in range(2, nh):
         low_grad = low_grad + low_grad_part(h)
     LG[...] = low_grad.astype(BF16)
@@ -829,19 +831,26 @@
         for t in range(1, ndp):
             total = total + RR[t, i].astype(F32)
         ZD[mz, i] = total.astype(BF16)
-        share(ZD.at[mz, i], 2 + i)
+        share(ZD.at[mz, i], 3 + i)
 
     zero = jnp.zeros((rows, 1), F32)
-    first, second = lax.fori_loop(0, ndp, hidden_body, (zero, zero))
+    middle = ndp // 2
+
+    def share_sums(i):
+        ZM[i, mz, pl.ds(0, 2)] = ZL[0:2, i * middle : (i + 1) * middle].astype(BF16)
+        share(ZM.at[i, mz, pl.ds(0, 2)], 5 + i)
+
+    sums = lax.fori_loop(0, middle, hidden_body, (zero, zero))
+    share_sums(0)
+    first, second = lax.fori_loop(middle, ndp, hidden_body, sums)
     wait_all(up_copies)
     up_sum = US[me].astype(F32)
     for t in range(1, ndp):
         up_sum = up_sum + UR[t].astype(F32)
     ZU[mz] = up_sum.astype(BF16)
-    share(ZU.at[mz], 1)
+    share(ZU.at[mz], 2)
     share_down(0)
-    ZM[mz, pl.ds(0, 2)] = ZL[0:2].astype(BF16)
-    share(ZM.at[mz, pl.ds(0, 2)], 4)
+    share_sums(1)
     first, second = first / width, second / width
 
     def last_body(j, _):
@@ -852,17 +861,20 @@
     lax.fori_loop(0, ndp, last_body, 0)
     share_down(1)
     wait_all(z_copies)
-    down_all, up_all, mod_all = ZD[0].astype(F32), ZU[0].astype(F32), ZM[0].astype(F32)
+    down_all, up_all = ZD[0].astype(F32), ZU[0].astype(F32)
     for z in range(1, nctx):
         down_all = down_all + ZD[z].astype(F32)
         up_all = up_all + ZU[z].astype(F32)
-        mod_all = mod_all + ZM[z].astype(F32)
     for i in range(2):
         down_out[i * half : (i + 1) * half, :] = down_all[i]
     up_out[...] = up_all
     for j in range(ndp):
+        mod_all = ZM[j // middle, 0].astype(F32)
+        for z in range(1, nctx):
+            mod_all = mod_all + ZM[j // middle, z].astype(F32)
+        row = j % middle
         for i in range(3):
-            mod_out[i, :, j * block : (j + 1) * block] = mod_all[i, j : j + 1, :]
+            mod_out[i, :, j * block : (j + 1) * block] = mod_all[i, row : row + 1, :]
 
     for k in range(items):
         used = range(10) if k in NEAR else (2, 4, 5, 6) if k in FAR else range(7)
@@ -926,14 +938,14 @@
         pltpu.VMEM((ndp, ur, hw), BF16),
         pltpu.VMEM((nctx, 2, rank2 // 2, block), BF16),
         pltpu.VMEM((nctx, ur, hw), BF16),
-        pltpu.VMEM((nctx, 3, ndp, block), BF16),
+        pltpu.VMEM((2, nctx, 3, ndp // 2, block), BF16),
         pltpu.VMEM((3, ndp, block), F32),
         sem((3,)),
         sem((3 * nh + 3,)),
         sem((10, 4 * nh + 2)),
         sem((8, 4 * nh + 2)),
     ]
-    scratch += [sem((nh, nctx))] * 8 + [sem((2, ndp))] * 2 + [sem((ndp,))] * 2 + [sem((5, nctx))] * 2
+    scratch += [sem((nh, nctx))] * 8 + [sem((2, ndp))] * 2 + [sem((ndp,))] * 2 + [sem((7, nctx))] * 2
     results = pl.pallas_call(
         functools.partial(layer_kernel, dims),
         out_shape=(

time: 81.5 us -> 81.1 us (level)
  no operation moved by 1% of the time
where the time goes in v4:
time: 81.1 us; the launch traced here: 81 us
  Pallas kernels  80.3 us (99%)
    pallas_call x1, Pallas kernels, per_device_kernel(): pl.pallas_call(functools.partial(layer_kernel, dims), out_shape=(pltpu.VM...  79.1 us

profile of v4, /device:TPU:0, one launch (start us, length us, event | category | flops | bytes accessed | tf_op | source)
XLA Modules:
  0.0 81.0 jit_solution(6775374395003860770)
XLA Ops:
  0.6 79.1 %shard_map.110 = (bf16[128,3072]{1,0:T(8,128)(2,1)S(1)}, bf16[128,3072]{1,0:T(8,128)(2,1)S(1)}, f32[3,1,3072]{2,1,0:T(1,128)S(1)}, f32[64,384]{1,0:T(8,128)S(1)}, f32[8,512]{1,0:T(8,128)S(1)}) custom-call(bf16[128,3072]{1,0:T(8,128)(2,1)} %bitcast.8, f32[3,1,3072]{2,1,0:T(1,128)} %bitcast.11, bf16[128,3072]{1,0:T(8,128)(2,1)} %bitcast.9, ...), custom_call_target="tpu_custom_call" | custom-call | tf_op jit(solution)/shard_map/pallas_call | solution.py:949
  79.8 1.2 %shard_map.111 = (bf16[128,3072]{1,0:T(8,128)(2,1)}, bf16[128,3072]{1,0:T(8,128)(2,1)}, f32[3,1,3072]{2,1,0:T(1,128)}, f32[64,384]{1,0:T(8,128)}, f32[8,512]{1,0:T(8,128)}) custom-call(bf16[128,3072]{1,0:T(8,128)(2,1)S(1)} %get-tuple-element.15.refs_0_, bf16[128,3072]{1,0:T(8,128)(2,1)S(1)} %get-tuple-element.16.refs_1_, ...), custom_call_target="tpu_custom_call" | custom-call | tf_op jit(solution)/shard_map/pallas_call | solution.py:973
